TPU v7x, 256 devices: a whole 4x4x8 slice. The times are simulated.
256 devices in a mesh: pipe: 2 (over core), seq: 16 (over z, x_hi), tp: 8 (over y, x_lo).
Axes of the slice: x: 4 (x_hi: 2, x_lo: 2; x = x_hi * 2 + x_lo), y: 4, z: 8, core: 2. Of those that a mesh axis runs over, the one named last changes fastest.
Arguments:
- hidden_in: bfloat16 [1, 8192, 2560], P(None, ('seq', 'tp')), may hold values from -6 to 6
- doc_ids: int32 [1, 8192], P(None, 'seq'), may hold values from 0 to 1, never falling along the last dimension, each value on 1 to 6144 neighbouring positions
- norm_gain: float32 [2, 2560], P('pipe'), may hold values from 0.1 to 1.9
- in_zx: bfloat16 [2, 2560, 2, 5120], P('pipe', None, None, 'tp'), may hold values from -0.125 to 0.125
- in_bc: bfloat16 [2, 2560, 256], P('pipe'), may hold values from -0.125 to 0.125
- in_dt: bfloat16 [2, 2560, 80], P('pipe', None, 'tp'), may hold values from -0.125 to 0.125
- conv_x: float32 [2, 4, 5120], P('pipe', None, 'tp'), may hold values from -3 to 3
- conv_bc: float32 [2, 4, 256], P('pipe'), may hold values from -3 to 3
- bias_x: float32 [2, 5120], P('pipe', 'tp'), may hold values from -3 to 3
- bias_bc: float32 [2, 256], P('pipe'), may hold values from -3 to 3
- dt_bias: float32 [2, 80], P('pipe', 'tp'), may hold values from -2 to 1
- a_log: float32 [2, 80], P('pipe', 'tp'), may hold values from -12 to 0, as said below
- d_skip: float32 [2, 80], P('pipe', 'tp'), may hold values from 0.5 to 1.5
- gated_gain: float32 [2, 5120], P('pipe', 'tp'), may hold values from 0.1 to 1.9
- out_w: bfloat16 [2, 5120, 2560], P('pipe', 'tp'), may hold values from -0.078125 to 0.078125
Outputs:
- section_out: bfloat16 [2, 1, 8192, 2560], P('pipe', None, ('seq', 'tp'))
Inputs may be any that keep to these rules, and one draw needn't show every extreme that they name: `doc_ids`: in each row the document numbers start at 0, never fall, and rise by one where a new document begins; every document spans 1 to 6144 positions. `a_log`: logarithms of rates between 0.5 / 8192 and 1.
All inputs are finite; a program needn't handle non-finite values.
Results may differ from a plain program's by a relative error of at most 0.02.
Values may be sent and summed in bfloat16 or wider, within the bound.
A program may use at most 128 MiB of HBM per device.

v0:
```python
import jax
import jax.numpy as jnp
from jax import lax
from jax.sharding import Mesh
from jax.sharding import PartitionSpec as P

BLOCK = 256
SEQ = ("seq_0", "seq_1")
TP = ("tp_0", "tp_1")
SEQ_TP = ("seq_0", "seq_1", "tp_0", "tp_1")


epsilon = 1e-05


def shifted(block, axis, distance):
    devices = range(lax.axis_size(axis))
    route = [(i - distance, i) for i in devices if i - distance in devices]
    return lax.ppermute(block, axis, route)


def filled_with(x, identity):
    return jax.tree.map(
        lambda a, e: jnp.broadcast_to(jnp.asarray(e, a.dtype), a.shape), x, identity
    )


def prefix_by_axis(x, axes, combine, identity):
    before = start = filled_with(x, identity)
    running = x
    for axis in reversed(axes):
        count, mine = (lax.axis_size(axis), lax.axis_index(axis))
        pieces = jax.tree.map(lambda part: lax.all_gather(part, axis), running)
        inside, running = (start, start)
        for k in range(count):
            passed = k < mine
            running = combine(running, jax.tree.map(lambda part: part[k], pieces))
            inside = jax.tree.map(lambda new, old: jnp.where(passed, new, old), running, inside)
        before = combine(inside, before)
    return before


def from_everyone(x, axis):
    copies = jnp.broadcast_to(x, (lax.axis_size(axis), *x.shape))
    return lax.all_to_all(copies, axis, split_axis=0, concat_axis=0, tiled=True)


def over_copies(x, axis):
    return from_everyone(x, axis).sum(axis=0)


def laid_out(blocks, dim):
    blocks = jnp.moveaxis(blocks, 0, dim)
    lengths = blocks.shape
    return blocks.reshape(*lengths[:dim], lengths[dim] * lengths[dim + 1], *lengths[dim + 2 :])


def collect(x, axis, dim):
    return laid_out(from_everyone(x, axis), dim)


def sum_by_axis(terms, axes):
    running = terms.astype(jnp.bfloat16)
    for axis in axes:
        running = lax.psum_scatter(running, axis, scatter_dimension=0, tiled=True)
    return running.astype(jnp.float32)


def conv_mix(row_block, edge_rows, row_ids, edge_ids, weight, shift_bias):
    padded = jnp.concatenate([edge_rows, row_block], 0)
    padded_ids = jnp.concatenate([edge_ids, row_ids], 0)
    row_count = row_block.shape[0]
    running = jnp.zeros_like(row_block) + shift_bias[None, :]
    for offset in range(weight.shape[0]):
        keep_mask = (padded_ids[offset : offset + row_count] == row_ids).astype(jnp.float32)
        running = (
            running
            + keep_mask[:, None] * weight[offset][None, :] * padded[offset : offset + row_count]
        )
    return jax.nn.silu(running)


def block_step(state_in, inputs, decay_rates):
    x_block, step_sizes, b_block, c_block, seg_block, prev_id = inputs
    log_decay = jnp.cumsum(step_sizes * decay_rates[:, None], axis=1)
    block_length = seg_block.shape[0]
    causal_mask = jnp.arange(block_length)[:, None] >= jnp.arange(block_length)[None, :]
    same_doc = causal_mask & (seg_block[:, None] == seg_block[None, :])
    spread = log_decay[:, :, None] - log_decay[:, None, :]
    mixing = jnp.where(same_doc[None], jnp.exp(jnp.where(same_doc[None], spread, 0.0)), 0.0)
    gram_matrix = jnp.dot(c_block, b_block.T)
    weights = mixing * gram_matrix[None] * step_sizes[:, None, :]
    outputs = jnp.einsum("hps,hts->hpt", x_block, weights)
    carried = (seg_block == prev_id).astype(jnp.float32)
    outputs = outputs + jnp.exp(log_decay)[:, None, :] * carried[None, None, :] * jnp.einsum(
        "hpn,tn->hpt", state_in, c_block
    )
    end_weight = (
        jnp.exp(log_decay[:, -1:] - log_decay)
        * (seg_block == seg_block[-1]).astype(jnp.float32)[None, :]
        * step_sizes
    )
    fresh_state = jnp.einsum("hps,sn->hpn", x_block * end_weight[:, None, :], b_block)
    keep_all = jnp.exp(log_decay[:, -1]) * (seg_block[-1] == prev_id).astype(jnp.float32)
    return (keep_all[:, None, None] * state_in + fresh_state, outputs)


def combine_carry(earlier, latter):
    return (earlier[0] * latter[0], latter[0][:, None, None] * earlier[1] + latter[1])


def rms_rows(hidden_f, norm_scale):
    return (
        hidden_f
        * lax.rsqrt(jnp.mean(hidden_f * hidden_f, axis=1, keepdims=True) + epsilon)
        * norm_scale[None, :]
    ).astype(jnp.bfloat16)


def project_rows(normed, weight_zx, weight_bc, weight_dt):
    return jnp.concatenate(
        [
            jnp.dot(normed, weight_zx, preferred_element_type=jnp.float32),
            jnp.dot(normed, weight_bc, preferred_element_type=jnp.float32),
            jnp.dot(normed, weight_dt, preferred_element_type=jnp.float32),
        ],
        1,
    )


def mixer_block(
    projected, row_ids, kernel, kernel_bias, dt_shift, log_rate, skip_scale, gate_scale
):
    local_width = gate_scale.shape[0]
    heads_local = dt_shift.shape[0]
    head_width = local_width // heads_local
    token_count = projected.shape[0]
    state_width = (kernel.shape[1] - local_width) // 2
    edge_count = kernel.shape[0] - 1
    gate_in = projected[:, :local_width]
    pre_conv = projected[:, local_width : 2 * local_width + 2 * state_width]
    dt_raw = projected[:, 2 * local_width + 2 * state_width :]
    edge_rows, edge_ids = shifted(
        (pre_conv[token_count - edge_count :], row_ids[token_count - edge_count :]), SEQ, 1
    )
    conv_out = conv_mix(pre_conv, edge_rows, row_ids, edge_ids, kernel, kernel_bias)
    x_heads = conv_out[:, :local_width].T.reshape(heads_local, head_width, token_count)
    b_conv = conv_out[:, local_width : local_width + state_width]
    c_conv = conv_out[:, local_width + state_width :]
    step_sizes = jax.nn.softplus(dt_raw + dt_shift[None, :]).T
    decay_rates = -jnp.exp(log_rate)
    first_prev = edge_ids[edge_count - 1]
    state_run = jnp.zeros((heads_local, head_width, state_width), jnp.float32)
    pieces = []
    for block_index in range(token_count // BLOCK):
        block_begin = block_index * BLOCK
        block_end = block_begin + BLOCK
        prev_id = first_prev if block_index == 0 else row_ids[block_begin - 1]
        state_run, block_out = block_step(
            state_run,
            (
                x_heads[:, :, block_begin:block_end],
                step_sizes[:, block_begin:block_end],
                b_conv[block_begin:block_end],
                c_conv[block_begin:block_end],
                row_ids[block_begin:block_end],
                prev_id,
            ),
            decay_rates,
        )
        pieces.append(block_out)
    outputs = jnp.concatenate(pieces, 2)
    log_total = jnp.cumsum(step_sizes * decay_rates[:, None], axis=1)
    carried = (row_ids == first_prev).astype(jnp.float32)
    shard_keep = jnp.exp(log_total[:, -1]) * carried[token_count - 1]
    prefix_keep, incoming = prefix_by_axis(
        (shard_keep, state_run),
        SEQ,
        combine_carry,
        (jnp.ones_like(shard_keep), jnp.zeros_like(state_run)),
    )
    outputs = outputs + jnp.exp(log_total)[:, None, :] * carried[None, None, :] * jnp.einsum(
        "hpn,tn->hpt", incoming, c_conv
    )
    outputs = outputs + skip_scale[:, None, None] * x_heads
    gated_rows = outputs.reshape(local_width, token_count).T * jax.nn.silu(gate_in)
    total_sq = over_copies(jnp.sum(gated_rows * gated_rows, axis=1), TP)
    full_width = local_width * lax.axis_size(TP)
    return (
        gated_rows * lax.rsqrt(total_sq / full_width + epsilon)[:, None] * gate_scale[None, :]
    ).astype(jnp.bfloat16)


def local(
    hidden_in,
    doc_ids,
    norm_gain,
    in_zx,
    in_bc,
    in_dt,
    conv_x,
    conv_bc,
    bias_x,
    bias_bc,
    dt_bias,
    a_log,
    d_skip,
    gated_gain,
    out_w,
):
    sections = lax.axis_size("pipe")
    section_index = lax.axis_index("pipe")
    micro_count = hidden_in.shape[0]
    local_width = gated_gain.shape[1]
    weight_zx = in_zx[0].reshape(in_zx.shape[1], 2 * local_width)
    weight_bc = in_bc[0]
    weight_dt = in_dt[0]
    kernel = jnp.concatenate([conv_x[0], conv_bc[0]], 1)
    kernel_bias = jnp.concatenate([bias_x[0], bias_bc[0]], 0)
    weight_out = out_w[0]
    saved_slots = [jnp.zeros_like(hidden_in[0])]
    received = jnp.zeros_like(hidden_in[0])
    finished = received
    for tick_index in range(micro_count + sections - 1):
        if tick_index > 0:
            received = shifted(finished, "pipe", 1)
        fresh_rows = hidden_in[tick_index] if tick_index < micro_count else jnp.zeros_like(received)
        current = jnp.where(section_index == 0, fresh_rows, received)
        micro_index = tick_index - section_index
        row_ids = lax.dynamic_index_in_dim(
            doc_ids, jnp.clip(micro_index, 0, micro_count - 1), 0, keepdims=False
        ).astype(jnp.float32)
        current_f = current.astype(jnp.float32)
        normed = rms_rows(current_f, norm_gain[0])
        projected = project_rows(collect(normed, TP, 0), weight_zx, weight_bc, weight_dt)
        branch_in = mixer_block(
            projected, row_ids, kernel, kernel_bias, dt_bias[0], a_log[0], d_skip[0], gated_gain[0]
        )
        branch = sum_by_axis(jnp.dot(branch_in, weight_out, preferred_element_type=jnp.float32), TP)
        finished = (current_f + branch).astype(jnp.bfloat16)
        saved_slots[0] = jnp.where(micro_index == 0, finished, saved_slots[0])
    stacked = jnp.stack(saved_slots)
    return stacked[None]


def solution(mesh):
    torus = Mesh(
        mesh.devices.reshape(mesh.shape["pipe"], 8, 2, 4, 2),
        ("pipe", "seq_0", "seq_1", "tp_0", "tp_1"),
    )
    in_specs = (
        P(None, SEQ_TP, None),
        P(None, SEQ),
        P("pipe", None),
        P("pipe", None, None, TP),
        P("pipe", None, None),
        P("pipe", None, TP),
        P("pipe", None, TP),
        P("pipe", None, None),
        P("pipe", TP),
        P("pipe", None),
        P("pipe", TP),
        P("pipe", TP),
        P("pipe", TP),
        P("pipe", TP),
        P("pipe", TP, None),
    )
    out_specs = P("pipe", None, SEQ_TP, None)
    return jax.shard_map(local, mesh=torus, in_specs=in_specs, out_specs=out_specs, check_vma=False)
```

profile of v0, /device:TPU:1, one launch (start us, length us, event | category | flops | bytes accessed | tf_op | source)
XLA Modules:
  0.0 464.8 jit_solution(12041885855625163148)
XLA Ops:
  7.8 1.8 broadcast_in_dim.50
  9.6 6.1 %all-to-all-start = ((bf16[8,64,2560]{2,1,0:T(8,128)(2,1)}), bf16[8,64,2560]{2,1,0:T(8,128)(2,1)}, u32[]{:S(2)}, u32[]{:S(2)}) async-start(bf16[8,64,2560]{2,1,0:T(8,128)(2,1)} %broadcast_in_dim.50), calls=%async_computation | async-start | bytes 5242880 | tf_op jit(solution)/shard_map/all_to_all | solution.py:45
  15.8 4.3 collective-permute-start
  20.2 6.8 %copy.134 = bf16[320,8,2,640]{3,1,2,0:T(8,128)(2,1)} copy(bf16[320,8,2,640]{3,2,1,0:T(2,128)(2,1)} %bitcast.280) | data formatting | bytes 13107200
  31.6 9.3 %collective-permute-done = f32[3]{0:T(128)S(1)} collective-permute-done((f32[3]{0:T(128)S(1)}, f32[3]{0:T(128)S(1)}, u32[]{:S(2)}, u32[]{:S(2)}) %collective-permute-start) | collective-permute-done | bytes 44 | tf_op jit(solution)/shard_map/ppermute | solution.py:19
  44.7 2.5 compare_convert_fusion
  47.2 2.5 broadcast_multiply_fusion.1
  51.7 7.3 %fusion.302 = f32[512,1280]{1,0:T(8,128)S(1)} fusion(bf16[512,2560]{1,0:T(8,128)(2,1)} %bitcast.7, bf16[2560,1280]{1,0:T(8,128)(2,1)} %bitcast.281), kind=kOutput, calls=%fused_computation.429 | convolution fusion | flops 3355443200 | bytes 11796480 | tf_op jit(solution)/shard_map/dot_general | solution.py:123
  59.0 3.5 fusion.48
  63.4 6.2 %collective-permute-start.1 = (f32[3,896]{1,0:T(4,128)}, f32[3,896]{1,0:T(4,128)}, u32[]{:S(2)}, u32[]{:S(2)}) collective-permute-start(f32[3,896]{1,0:T(4,128)} %pad_maximum_fusion.5), channel_id=1, source_target_pairs={{0,8},{8,16},{16,24},{24,32},{32,40},{40,48},{48,56},{56,64},{64,7... | collective-permute-start | bytes 32264 | tf_op jit(solution)/shard_map/ppermute | solution.py:19
  72.1 5.8 %all-reduce = f32[20]{0:T(128)} all-reduce(f32[20]{0:T(128)S(1)} %dynamic-update-slice), channel_id=2, replica_groups=mesh['pipe'=2,'seq_0'=8,'seq_1'=2,'tp_0'=4,'tp_1'=2] {'seq_1'}, use_global_device_ids=true, to_apply=%add | all-reduce | flops 20 | bytes 160
  83.6 2.6 divide_multiply_fusion.1
  88.7 2.8 copy.111
  94.9 8.1 %all-gather.1 = f32[20,64,128]{2,1,0:T(8,128)S(1)} all-gather(f32[10,64,128]{2,1,0:T(8,128)S(1)} %convolution_add_fusion.2), channel_id=3, replica_groups=mesh['pipe'=2,'seq_0'=8,'seq_1'=2,'tp_0'=4,'tp_1'=2] {'seq_1'}, dimensions={0}, use_global_device_ids=true | all-gather | bytes 983040 | tf_op jit(solution)/shard_map/all_gather | solution.py:33
  106.2 16.5 %all-reduce.1 = f32[80]{0:T(128)S(1)} all-reduce(f32[80]{0:T(128)S(1)} %get-tuple-element.55), channel_id=6, replica_groups=mesh['pipe'=2,'seq_0'=8,'seq_1'=2,'tp_0'=4,'tp_1'=2] {'seq_0'}, use_global_device_ids=true, to_apply=%add.1 | all-reduce | flops 80 | bytes 640
  125.8 2.2 fusion.23
  128.0 2.0 fusion.77
  131.0 2.0 fusion.76
  133.0 17.7 %all-gather.9.cloned.1.call-done = f32[8,10,64,128]{3,2,1,0:T(8,128)} async-done(((f32[1,10,64,128]{3,2,1,0:T(8,128)}), f32[8,10,64,128]{3,2,1,0:T(8,128)}) %all-gather.9.cloned.1.call-update) | async-done | bytes 2621456 | tf_op jit(solution)/shard_map/all_gather | solution.py:33
  150.7 4.6 fusion.45
  155.4 2.8 copy.118
  158.2 2.2 multiply_reduce_fusion.1
  161.0 4.9 %all-to-all-start.1 = ((f32[8,1,512]{2,1,0:T(1,128)}), f32[8,1,512]{2,1,0:T(1,128)S(1)}, u32[]{:S(2)}, u32[]{:S(2)}) async-start(f32[8,1,512]{2,1,0:T(1,128)} %broadcast_in_dim.54), calls=%async_computation.1 | async-start | bytes 32768 | tf_op jit(solution)/shard_map/all_to_all | solution.py:45
  166.0 5.0 %all-to-all-done.1 = f32[8,1,512]{2,1,0:T(1,128)S(1)} async-done(((f32[8,1,512]{2,1,0:T(1,128)}), f32[8,1,512]{2,1,0:T(1,128)S(1)}, u32[]{:S(2)}, u32[]{:S(2)}) %all-to-all-start.1) | async-done | bytes 16416 | tf_op jit(solution)/shard_map/all_to_all | solution.py:45
  171.0 5.6 %convolution_convert_fusion.1 = bf16[512,2560]{1,0:T(8,128)(2,1)} fusion(bf16[1,640,2560]{2,1,0:T(8,128)(2,1)S(1)} %copy-done, f32[640]{0:T(1024)S(1)} %reduce.14, f32[512]{0:T(512)S(1)} %add_rsqrt_fusion.1, f32[640,512]{0,1:T(8,128)} %copy.118, f32[512,1280]{1,0:T(8,128)} %copy-done.1), kind=kOutput, calls=%fused_computation.1 | convolution fusion | flops 1681653760 | bytes 8524288 | tf_op jit(solution)/shard_map/dot_general | solution.py:239
  176.7 37.7 %reduce-scatter.5.cloned.1.call-done = bf16[128,2560]{1,0:T(8,128)(2,1)} async-done(((bf16[512,2560]{1,0:T(8,128)(2,1)}), bf16[128,2560]{1,0:T(8,128)(2,1)}) %reduce-scatter.5.cloned.1.call-update) | async-done | bytes 655376 | tf_op jit(solution)/shard_map/reduce_scatter | solution.py:65
  214.5 23.2 %reduce-scatter.7.cloned.1.call-done = bf16[64,2560]{1,0:T(8,128)(2,1)} async-done(((bf16[128,2560]{1,0:T(8,128)(2,1)}), bf16[64,2560]{1,0:T(8,128)(2,1)}) %reduce-scatter.7.cloned.1.call-update) | async-done | bytes 327696 | tf_op jit(solution)/shard_map/reduce_scatter | solution.py:65
  240.1 2.2 collective-permute-done.2
  243.3 36.0 %all_to_all.22 = bf16[8,64,2560]{2,1,0:T(8,128)(2,1)S(1)} all-to-all(bf16[8,64,2560]{2,1,0:T(8,128)(2,1)S(1)} %broadcast_in_dim.55), channel_id=1, replica_groups=mesh['pipe'=2,'seq_0'=8,'seq_1'=2,'tp_0'=4,'tp_1'=2] {'tp_0','tp_1'}, dimensions={0} | all-to-all | bytes 5242880 | tf_op jit(solution)/shard_map/all_to_all | solution.py:45
  279.4 8.1 %fusion.303 = f32[512,1280]{1,0:T(8,128)} fusion(bf16[512,2560]{1,0:T(8,128)(2,1)S(1)} %bitcast.277, bf16[2560,1280]{1,0:T(8,128)(2,1)} %bitcast.282), kind=kOutput, calls=%fused_computation.430 | convolution fusion | flops 3355443200 | bytes 11796480 | tf_op jit(solution)/shard_map/dot_general | solution.py:123
  294.3 5.2 %collective-permute-start.3 = (f32[3,896]{1,0:T(4,128)}, f32[3,896]{1,0:T(4,128)}, u32[]{:S(2)}, u32[]{:S(2)}) collective-permute-start(f32[3,896]{1,0:T(4,128)} %pad_maximum_fusion.4), channel_id=1, source_target_pairs={{0,8},{8,16},{16,24},{24,32},{32,40},{40,48},{48,56},{56,64},{64,7... | collective-permute-start | bytes 32264 | tf_op jit(solution)/shard_map/ppermute | solution.py:19
  302.0 5.3 %all-reduce.2 = f32[20]{0:T(128)S(1)} all-reduce(f32[20]{0:T(128)S(1)} %dynamic-update-slice.2), channel_id=4, replica_groups=mesh['pipe'=2,'seq_0'=8,'seq_1'=2,'tp_0'=4,'tp_1'=2] {'seq_1'}, use_global_device_ids=true, to_apply=%add.2 | all-reduce | flops 20 | bytes 160
  309.5 2.6 divide_multiply_fusion
  314.5 2.8 copy.121
  320.8 8.8 %all-gather.3 = f32[20,64,128]{2,1,0:T(8,128)S(1)} all-gather(f32[10,64,128]{2,1,0:T(8,128)S(1)} %convolution_add_fusion), channel_id=5, replica_groups=mesh['pipe'=2,'seq_0'=8,'seq_1'=2,'tp_0'=4,'tp_1'=2] {'seq_1'}, dimensions={0}, use_global_device_ids=true | all-gather | bytes 983040 | tf_op jit(solution)/shard_map/all_gather | solution.py:33
  331.4 13.1 %all-reduce.3 = f32[80]{0:T(128)S(1)} all-reduce(f32[80]{0:T(128)S(1)} %get-tuple-element.43), channel_id=7, replica_groups=mesh['pipe'=2,'seq_0'=8,'seq_1'=2,'tp_0'=4,'tp_1'=2] {'seq_0'}, use_global_device_ids=true, to_apply=%add.3 | all-reduce | flops 80 | bytes 640
  347.6 2.1 fusion.9
  349.7 2.0 fusion.75
  352.9 2.0 fusion.74
  354.8 15.3 %all-gather.11.cloned.1.call-done = f32[8,10,64,128]{3,2,1,0:T(8,128)} async-done(((f32[1,10,64,128]{3,2,1,0:T(8,128)}), f32[8,10,64,128]{3,2,1,0:T(8,128)}) %all-gather.11.cloned.1.call-update) | async-done | bytes 2621456 | tf_op jit(solution)/shard_map/all_gather | solution.py:33
  370.3 4.5 fusion.44
  374.8 2.8 copy.128
  377.6 2.2 multiply_reduce_fusion
  379.8 9.7 %all_to_all.23 = f32[8,1,512]{2,1,0:T(1,128)S(1)} all-to-all(f32[8,1,512]{2,1,0:T(1,128)S(1)} %broadcast_in_dim.56), channel_id=1, replica_groups=mesh['pipe'=2,'seq_0'=8,'seq_1'=2,'tp_0'=4,'tp_1'=2] {'tp_0','tp_1'}, dimensions={0} | all-to-all | bytes 32768 | tf_op jit(solution)/shard_map/all_to_all | solution.py:45
  389.6 5.7 %convolution_convert_fusion = bf16[512,2560]{1,0:T(8,128)(2,1)} fusion(bf16[1,640,2560]{2,1,0:T(8,128)(2,1)S(1)} %copy-done, f32[512]{0:T(512)S(1)} %add_rsqrt_fusion, f32[640]{0:T(1024)S(1)} %copy-done.46, f32[640,512]{0,1:T(8,128)} %copy.128, f32[512,1280]{1,0:T(8,128)} %fusion.303), kind=kOutput, calls=%fused_computation | convolution fusion | flops 1681653760 | bytes 8524288 | tf_op jit(solution)/shard_map/dot_general | solution.py:239
  395.4 37.5 %reduce-scatter.9.cloned.1.call-done = bf16[128,2560]{1,0:T(8,128)(2,1)} async-done(((bf16[512,2560]{1,0:T(8,128)(2,1)}), bf16[128,2560]{1,0:T(8,128)(2,1)}) %reduce-scatter.9.cloned.1.call-update) | async-done | bytes 655376 | tf_op jit(solution)/shard_map/reduce_scatter | solution.py:65
  432.9 23.1 %reduce-scatter.11.cloned.1.call-done = bf16[64,2560]{1,0:T(8,128)(2,1)} async-done(((bf16[128,2560]{1,0:T(8,128)(2,1)}), bf16[64,2560]{1,0:T(8,128)(2,1)}) %reduce-scatter.11.cloned.1.call-update) | async-done | bytes 327696 | tf_op jit(solution)/shard_map/reduce_scatter | solution.py:65
  456.0 2.0 fusion.105
  (321 shorter events, 57.0 us)
Async XLA Ops:
  6.5 164.5 %copy-start = (bf16[1,640,2560]{2,1,0:T(8,128)(2,1)S(1)}, bf16[1,640,2560]{2,1,0:T(8,128)(2,1)}, u32[]{:S(2)}) copy-start(bf16[1,640,2560]{2,1,0:T(8,128)(2,1)} %param.29) | copy-start | bytes 9830404
  9.6 37.6 %all-to-all-start = ((bf16[8,64,2560]{2,1,0:T(8,128)(2,1)}), bf16[8,64,2560]{2,1,0:T(8,128)(2,1)}, u32[]{:S(2)}, u32[]{:S(2)}) async-start(bf16[8,64,2560]{2,1,0:T(8,128)(2,1)} %broadcast_in_dim.50), calls=%async_computation | async-start | bytes 5242880 | tf_op jit(solution)/shard_map/all_to_all | solution.py:45
  15.6 135.1 %all-gather.9.cloned.1.call-start = ((), (), s32[]{:S(2)}) async-start(), calls=%async_computation.8 | async-start | bytes 2949120 | tf_op jit(solution)/shard_map/all_gather | solution.py:33
  15.8 25.1 %collective-permute-start = (f32[3]{0:T(128)S(1)}, f32[3]{0:T(128)S(1)}, u32[]{:S(2)}, u32[]{:S(2)}) collective-permute-start(f32[3]{0:T(128)S(1)} %slice_bitcast_fusion.22), channel_id=1, source_target_pairs={{0,8},{8,16},{16,24},{24,32},{32,40},{40,48},{48,56},{56,64},{64,7... | collective-permute-start | bytes 44 | tf_op jit(solution)/shard_map/ppermute | solution.py:19
  20.2 27.0 %copy-start.15 = (bf16[1,2560,10]{1,2,0:T(8,128)(2,1)S(1)}, bf16[1,2560,10]{1,2,0:T(8,128)(2,1)}, u32[]{:S(2)}) copy-start(bf16[1,2560,10]{1,2,0:T(8,128)(2,1)} %param.20) | copy-start | bytes 153604
  20.2 27.0 %copy-start.49 = (f32[1,10]{1,0:T(1,128)S(1)}, f32[1,10]{1,0:T(1,128)}, u32[]{:S(2)}) copy-start(f32[1,10]{1,0:T(1,128)} %param.25) | copy-start | bytes 124
  31.6 18.3 %copy-start.42 = (f32[10]{0:T(128)}, f32[10]{0:T(128)S(1)}, u32[]{:S(2)}) copy-start(f32[10]{0:T(128)S(1)} %negate_bitcast_fusion) | copy-start | bytes 124
  31.6 18.2 %copy-start.30 = (f32[1,256]{1,0:T(1,128)}, f32[1,256]{1,0:T(1,128)S(1)}, u32[]{:S(2)}) copy-start(f32[1,256]{1,0:T(1,128)S(1)} %get-tuple-element.36) | copy-start | bytes 3076
  31.6 19.2 %copy-start.32 = (f32[1,256]{1,0:T(1,128)}, f32[1,256]{1,0:T(1,128)S(1)}, u32[]{:S(2)}) copy-start(f32[1,256]{1,0:T(1,128)S(1)} %get-tuple-element.35) | copy-start | bytes 3076
  63.4 20.1 %collective-permute-start.1 = (f32[3,896]{1,0:T(4,128)}, f32[3,896]{1,0:T(4,128)}, u32[]{:S(2)}, u32[]{:S(2)}) collective-permute-start(f32[3,896]{1,0:T(4,128)} %pad_maximum_fusion.5), channel_id=1, source_target_pairs={{0,8},{8,16},{16,24},{24,32},{32,40},{40,48},{48,56},{56,64},{64,7... | collective-permute-start | bytes 32264 | tf_op jit(solution)/shard_map/ppermute | solution.py:19
  81.9 21.1 %copy-start.51 = (f32[10]{0:T(128)}, f32[10]{0:T(128)S(1)}, u32[]{:S(2)}) copy-start(f32[10]{0:T(128)S(1)} %get-tuple-element.54) | copy-start | bytes 124
  81.9 21.1 %copy-start.53 = (f32[10]{0:T(128)}, f32[10]{0:T(128)S(1)}, u32[]{:S(2)}) copy-start(f32[10]{0:T(128)S(1)} %get-tuple-element.56) | copy-start | bytes 124
  93.6 11.9 %copy-start.31 = (f32[1,256]{1,0:T(1,128)S(1)}, f32[1,256]{1,0:T(1,128)}, u32[]{:S(2)}) copy-start(f32[1,256]{1,0:T(1,128)} %copy-done.30) | copy-start | bytes 3076
  93.6 29.9 %copy-start.28 = (f32[512]{0:T(512)S(1)}, f32[512]{0:T(512)}, u32[]{:S(2)}) copy-start(f32[512]{0:T(512)} %copy-done.27) | copy-start | bytes 6148
  130.0 20.7 %copy-start.52 = (f32[10]{0:T(128)S(1)}, f32[10]{0:T(128)}, u32[]{:S(2)}) copy-start(f32[10]{0:T(128)} %copy-done.51) | copy-start | bytes 124
  130.0 20.7 %copy-start.54 = (f32[10]{0:T(128)S(1)}, f32[10]{0:T(128)}, u32[]{:S(2)}) copy-start(f32[10]{0:T(128)} %copy-done.53) | copy-start | bytes 124
  130.0 20.7 %copy-start.63 = (f32[10]{0:T(128)S(1)}, f32[10]{0:T(128)}, u32[]{:S(2)}) copy-start(f32[10]{0:T(128)} %get-tuple-element.53) | copy-start | bytes 124
  130.0 20.7 %copy-start.73 = (f32[10]{0:T(128)S(1)}, f32[10]{0:T(128)}, u32[]{:S(2)}) copy-start(f32[10]{0:T(128)} %get-tuple-element.57) | copy-start | bytes 124
  130.0 20.7 %copy-start.74 = (f32[10]{0:T(128)S(1)}, f32[10]{0:T(128)}, u32[]{:S(2)}) copy-start(f32[10]{0:T(128)} %get-tuple-element.58) | copy-start | bytes 124
  130.0 20.7 %copy-start.75 = (f32[10]{0:T(128)S(1)}, f32[10]{0:T(128)}, u32[]{:S(2)}) copy-start(f32[10]{0:T(128)} %get-tuple-element.59) | copy-start | bytes 124
  130.0 20.7 %copy-start.76 = (f32[10]{0:T(128)S(1)}, f32[10]{0:T(128)}, u32[]{:S(2)}) copy-start(f32[10]{0:T(128)} %get-tuple-element.60) | copy-start | bytes 124
  130.1 20.7 %copy-start.77 = (f32[10]{0:T(128)S(1)}, f32[10]{0:T(128)}, u32[]{:S(2)}) copy-start(f32[10]{0:T(128)} %get-tuple-element.61) | copy-start | bytes 124
  161.0 10.0 %all-to-all-start.1 = ((f32[8,1,512]{2,1,0:T(1,128)}), f32[8,1,512]{2,1,0:T(1,128)S(1)}, u32[]{:S(2)}, u32[]{:S(2)}) async-start(f32[8,1,512]{2,1,0:T(1,128)} %broadcast_in_dim.54), calls=%async_computation.1 | async-start | bytes 32768 | tf_op jit(solution)/shard_map/all_to_all | solution.py:45
  165.9 48.5 %reduce-scatter.5.cloned.1.call-start = ((), (), s32[]{:S(2)}) async-start(), calls=%async_computation.9 | async-start | bytes 3276800 | tf_op jit(solution)/shard_map/reduce_scatter | solution.py:65
  176.7 61.0 %reduce-scatter.7.cloned.1.call-start = ((), (), s32[]{:S(2)}) async-start(), calls=%async_computation.10 | async-start | bytes 983040 | tf_op jit(solution)/shard_map/reduce_scatter | solution.py:65
  214.4 155.8 %all-gather.11.cloned.1.call-start = ((), (), s32[]{:S(2)}) async-start(), calls=%async_computation.11 | async-start | bytes 2949120 | tf_op jit(solution)/shard_map/all_gather | solution.py:33
  238.8 3.5 collective-permute-start.2
  294.3 15.2 %collective-permute-start.3 = (f32[3,896]{1,0:T(4,128)}, f32[3,896]{1,0:T(4,128)}, u32[]{:S(2)}, u32[]{:S(2)}) collective-permute-start(f32[3,896]{1,0:T(4,128)} %pad_maximum_fusion.4), channel_id=1, source_target_pairs={{0,8},{8,16},{16,24},{24,32},{32,40},{40,48},{48,56},{56,64},{64,7... | collective-permute-start | bytes 32264 | tf_op jit(solution)/shard_map/ppermute | solution.py:19
  307.8 21.8 %copy-start.55 = (f32[10]{0:T(128)}, f32[10]{0:T(128)S(1)}, u32[]{:S(2)}) copy-start(f32[10]{0:T(128)S(1)} %get-tuple-element.42) | copy-start | bytes 124
  307.8 21.8 %copy-start.57 = (f32[10]{0:T(128)}, f32[10]{0:T(128)S(1)}, u32[]{:S(2)}) copy-start(f32[10]{0:T(128)S(1)} %get-tuple-element.44) | copy-start | bytes 124
  319.4 25.8 %copy-start.29 = (f32[512]{0:T(512)S(1)}, f32[512]{0:T(512)}, u32[]{:S(2)}) copy-start(f32[512]{0:T(512)} %copy-done.27) | copy-start | bytes 6148
  320.8 26.8 %copy-start.18 = (pred[256,256]{1,0:T(8,128)(4,1)S(1)}, pred[256,256]{1,0:T(8,128)(4,1)}, u32[]{:S(2)}) copy-start(pred[256,256]{1,0:T(8,128)(4,1)} %fusion.193) | copy-start | bytes 196612
  320.8 26.8 %copy-start.35 = (f32[10,256]{1,0:T(8,128)S(1)}, f32[10,256]{1,0:T(8,128)}, u32[]{:S(2)}) copy-start(f32[10,256]{1,0:T(8,128)} %get-tuple-element.16) | copy-start | bytes 30724
  331.4 101.6 %reduce-scatter.9.cloned.1.call-start = ((), (), s32[]{:S(2)}) async-start(), calls=%async_computation.12 | async-start | bytes 3276800 | tf_op jit(solution)/shard_map/reduce_scatter | solution.py:65
  351.8 18.4 %copy-start.56 = (f32[10]{0:T(128)S(1)}, f32[10]{0:T(128)}, u32[]{:S(2)}) copy-start(f32[10]{0:T(128)} %copy-done.55) | copy-start | bytes 124
  351.8 18.4 %copy-start.58 = (f32[10]{0:T(128)S(1)}, f32[10]{0:T(128)}, u32[]{:S(2)}) copy-start(f32[10]{0:T(128)} %copy-done.57) | copy-start | bytes 124
  351.8 18.4 %copy-start.64 = (f32[10]{0:T(128)S(1)}, f32[10]{0:T(128)}, u32[]{:S(2)}) copy-start(f32[10]{0:T(128)} %get-tuple-element.41) | copy-start | bytes 124
  351.8 18.4 %copy-start.65 = (f32[10]{0:T(128)S(1)}, f32[10]{0:T(128)}, u32[]{:S(2)}) copy-start(f32[10]{0:T(128)} %get-tuple-element.45) | copy-start | bytes 124
  351.8 18.4 %copy-start.66 = (f32[10]{0:T(128)S(1)}, f32[10]{0:T(128)}, u32[]{:S(2)}) copy-start(f32[10]{0:T(128)} %get-tuple-element.46) | copy-start | bytes 124
  351.8 18.4 %copy-start.67 = (f32[10]{0:T(128)S(1)}, f32[10]{0:T(128)}, u32[]{:S(2)}) copy-start(f32[10]{0:T(128)} %get-tuple-element.47) | copy-start | bytes 124
  351.8 18.4 %copy-start.68 = (f32[10]{0:T(128)S(1)}, f32[10]{0:T(128)}, u32[]{:S(2)}) copy-start(f32[10]{0:T(128)} %get-tuple-element.48) | copy-start | bytes 124
  351.8 18.4 %copy-start.69 = (f32[10]{0:T(128)S(1)}, f32[10]{0:T(128)}, u32[]{:S(2)}) copy-start(f32[10]{0:T(128)} %get-tuple-element.49) | copy-start | bytes 124
  351.9 18.4 %copy-start.70 = (f32[10]{0:T(128)S(1)}, f32[10]{0:T(128)}, u32[]{:S(2)}) copy-start(f32[10]{0:T(128)} %get-tuple-element.50) | copy-start | bytes 124
  351.9 18.4 %copy-start.71 = (f32[10]{0:T(128)S(1)}, f32[10]{0:T(128)}, u32[]{:S(2)}) copy-start(f32[10]{0:T(128)} %get-tuple-element.51) | copy-start | bytes 124
  351.9 18.4 %copy-start.72 = (f32[10]{0:T(128)S(1)}, f32[10]{0:T(128)}, u32[]{:S(2)}) copy-start(f32[10]{0:T(128)} %get-tuple-element.52) | copy-start | bytes 124
  351.9 18.4 %copy-start.81 = (f32[1,10]{1,0:T(1,128)S(1)}, f32[1,10]{1,0:T(1,128)}, u32[]{:S(2)}) copy-start(f32[1,10]{1,0:T(1,128)} %param.27) | copy-start | bytes 124
  377.6 12.0 %copy-start.46 = (f32[640]{0:T(1024)S(1)}, f32[640]{0:T(1024)}, u32[]{:S(2)}) copy-start(f32[640]{0:T(1024)} %copy-done.45) | copy-start | bytes 7684
  395.3 60.7 %reduce-scatter.11.cloned.1.call-start = ((), (), s32[]{:S(2)}) async-start(), calls=%async_computation.13 | async-start | bytes 983040 | tf_op jit(solution)/shard_map/reduce_scatter | solution.py:65
  (48 other events, 205.8 us)
Sparse Core Ops, SparseCore 0:
  104.9 45.7 all-gather.8
  176.8 37.5 reduce-scatter.4
  216.9 20.7 reduce-scatter.6
  331.5 38.6 all-gather.10
  395.4 37.4 reduce-scatter.8
  435.3 20.7 reduce-scatter.10
where the time goes:
time: 466 us; the launch traced here: 465 us
  waiting for transfers between devices  171 us (37%)
  blocking collectives  103 us (22%)
  matrix products  68.5 us (15%)
  other arithmetic  39.8 us (9%)
  local copies, waits for them, and re-layouts  35 us (8%)
  starting transfers between devices  28.3 us (6%)
  between operations  18.7 us (4%)
    reduce_scatter x4, waiting for transfers between devices, sum_by_axis(): running = lax.psum_scatter(running, axis, scatter_dimension=0, tiled=True)  122 us
    all_to_all x2, blocking collectives, from_everyone(): return lax.all_to_all(copies, axis, split_axis=0, concat_axis=0, tiled=True)  45.8 us
    unnamed x4, blocking collectives  40.7 us
    all_gather x2, waiting for transfers between devices, prefix_by_axis(): pieces = jax.tree.map(lambda part: lax.all_gather(part, axis), running)  33 us
    ppermute x4, starting transfers between devices, shifted(): return lax.ppermute(block, axis, route)  17 us
    all_gather x2, blocking collectives, prefix_by_axis(): pieces = jax.tree.map(lambda part: lax.all_gather(part, axis), running)  16.9 us
    dot_general x2, matrix products, project_rows(): jnp.dot(normed, weight_zx, preferred_element_type=jnp.float32)  15.4 us
    unnamed x189, local copies, waits for them, and re-layouts  15.3 us
  transfers between devices with their start and end apart: 12, of which 9 were waited for; matrix products, arithmetic and copies ran while one was open for 10% of the time, Pallas kernels for 0%

commit v1 on v0

v1 whole, which is shorter than its diff:
```python
import functools

import jax
import jax.numpy as jnp
from jax import lax
from jax.experimental import pallas as pl
from jax.experimental.pallas import tpu as pltpu
from jax.sharding import PartitionSpec as P

BLOCK = 256
EPS = 1e-05
F32 = jnp.float32
BF16 = jnp.bfloat16
MESH = pl.DeviceIdType.MESH


def lanes_of(v, spread):
    hi = v.astype(BF16)
    lo = (v - hi.astype(F32)).astype(BF16)
    return jnp.dot(hi, spread, preferred_element_type=F32) + jnp.dot(
        lo, spread, preferred_element_type=F32
    )


def layer_kernel(
    geo,
    hidden_hbm,
    ids_ref,
    norm_gain,
    zx_hbm,
    bc_hbm,
    dt_hbm,
    conv_x,
    conv_bc,
    bias_x,
    bias_bc,
    dt_bias,
    a_log,
    d_skip,
    gated_gain,
    out_hbm,
    result,
    w_zx,
    w_bc,
    w_dt,
    w_out,
    hid,
    rows_all,
    pre,
    gate,
    xc,
    bcm,
    xp,
    acc,
    idc,
    dtp,
    prm,
    ldb,
    st,
    a_out,
    a_in,
    k_out,
    k_in,
    i_out,
    i_in,
    part,
    xl_in,
    ql,
    yl2,
    yl1,
    yr2,
    yr1,
    qr,
    qx,
    xr_in,
    sq_out,
    sq_in,
    sqc,
    send_sem,
    recv_sem,
    load_sem,
):
    n_seq, n_tp, n_y, d, el, nh, cl = geo
    pipe, seq, tp = lax.axis_index("pipe"), lax.axis_index("seq"), lax.axis_index("tp")
    y, xl = tp // 2, tp % 2
    rows = hid.shape[0]
    toks = n_tp * rows
    half = rows // 2
    n_blocks = toks // BLOCK
    ng = 128 // n_seq
    up, down = lax.rem(y + 1, n_y), lax.rem(y + n_y - 1, n_y)
    far = lax.rem(y + 2, n_y)
    at_up = {"tp": up * 2 + xl}
    at_down = {"tp": down * 2 + xl}
    at_x = {"tp": y * 2 + (1 - xl)}
    left, right = pl.ds(0, cl), pl.ds(cl, d - cl)
    counter = [0]
    sent = []

    def remote(src, dst, where):
        k = counter[0]
        counter[0] += 1
        copy = pltpu.make_async_remote_copy(
            src_ref=src,
            dst_ref=dst,
            send_sem=send_sem.at[k],
            recv_sem=recv_sem.at[k],
            device_id=where,
            device_id_type=MESH,
        )
        return copy

    def push(src, dst, where):
        copy = remote(src, dst, where)
        copy.start()
        sent.append(copy)
        return copy

    loads = [
        pltpu.make_async_copy(s, t, load_sem.at[k])
        for k, (s, t) in enumerate(
            [(zx_hbm, w_zx), (bc_hbm, w_bc), (dt_hbm, w_dt), (out_hbm, w_out)]
        )
    ]
    first_load = pltpu.make_async_copy(hidden_hbm, hid, load_sem.at[4])

    @pl.when(pipe == 0)
    def _():
        first_load.start()

    for copy in loads:
        copy.start()

    barrier = pltpu.get_barrier_semaphore()
    pl.semaphore_signal(barrier, inc=1, device_id={"pipe": 1 - pipe}, device_id_type=MESH)
    for k in range(1, n_tp):
        pl.semaphore_signal(
            barrier, inc=1, device_id={"tp": lax.rem(tp + k, n_tp)}, device_id_type=MESH
        )
    for k in range(1, n_seq):
        pl.semaphore_signal(
            barrier, inc=1, device_id={"seq": lax.rem(seq + k, n_seq)}, device_id_type=MESH
        )

    prm[...] = jnp.zeros_like(prm)
    prm[0:1, 0:nh] = dt_bias[...]
    prm[1:2, 0:nh] = -jnp.exp(a_log[...])
    prm[2:3, 0:nh] = d_skip[...]
    ids_row = ids_ref[...].astype(F32)
    idc[8 : 8 + toks, :] = jnp.broadcast_to(ids_row, (128, toks)).T
    head = lax.broadcasted_iota(jnp.int32, (128, el), 0)
    lane = lax.broadcasted_iota(jnp.int32, (128, el), 1)
    spread = jnp.where((lane // 64) == head, 1.0, 0.0).astype(BF16)

    pl.semaphore_wait(barrier, n_tp + n_seq - 1)
    nxt = {"seq": lax.rem(seq + 1, n_seq)}
    id_edge = push(idc.at[pl.ds(toks, 8)], idc.at[pl.ds(0, 8)], nxt)
    handoff = remote(result, hid, {"pipe": 1 - pipe})

    @pl.when(pipe == 0)
    def _():
        first_load.wait()

    @pl.when(pipe == 1)
    def _():
        handoff.wait_recv()

    h = hid[...].astype(F32)
    scale = lax.rsqrt(jnp.mean(h * h, axis=1, keepdims=True) + EPS)
    rows_all[tp] = (h * scale * norm_gain[...]).astype(BF16)

    def slot(yy, xx, cols, r0=0, n=rows):
        return rows_all.at[yy * 2 + xx, pl.ds(r0, n), cols]

    def hop(yy, xx, cols, where, r0=0, n=rows):
        s = slot(yy, xx, cols, r0, n)
        return push(s, s, where)

    other = 1 - xl
    u1, d1 = hop(y, xl, left, at_up), hop(y, xl, left, at_down)
    x1 = hop(y, xl, right, at_x)
    u2, d2 = hop(y, xl, right, at_up), hop(y, xl, right, at_down)
    x2 = hop(y, xl, left, at_x)
    x1.wait_recv()
    u3, d3 = hop(y, other, right, at_up), hop(y, other, right, at_down)
    u1.wait_recv()
    u4 = hop(down, xl, left, at_up, 0, half)
    x3 = hop(down, xl, left, at_x)
    d1.wait_recv()
    d4 = hop(up, xl, left, at_down, half, half)
    x4 = hop(up, xl, left, at_x)
    u2.wait_recv()
    u3.wait_recv()
    u5 = hop(down, 0, right, at_up)
    d2.wait_recv()
    d3.wait_recv()
    d5 = hop(up, 1, right, at_down)
    u4.wait_recv()
    d4.wait_recv()
    x5 = hop(far, xl, left, at_x)
    id_edge.wait_recv()
    idc[0:8, :] = jnp.where(seq > 0, idc[0:8, :], -1.0)
    loads[0].wait()
    loads[1].wait()
    loads[2].wait()
    for copy in (x2, x3, x4, u5, d5, x5):
        copy.wait_recv()

    n_half = n_tp // 2
    m_half = n_half * rows

    def project(weight, w0, width, target, t0, r0):
        full = width // 256

        def tile(c0, w):
            for i in range(2):
                lhs = rows_all[n_half * i : n_half * (i + 1)].reshape(m_half, d)
                target[pl.ds(r0 + i * m_half, m_half), pl.ds(t0 + c0, w)] = jnp.dot(
                    lhs, weight[:, pl.ds(w0 + c0, w)], preferred_element_type=F32
                )

        def step(i, carry):
            tile(pl.multiple_of(i * 256, 256), 256)
            return carry

        lax.fori_loop(0, full, step, 0)
        if width % 256:
            tile(full * 256, width % 256)

    project(w_zx, el, el, pre, 0, 8)
    project(w_bc, 0, 256, pre, el, 8)
    dtp[...] = jnp.zeros_like(dtp)
    for i in range(2):
        lhs = rows_all[n_half * i : n_half * (i + 1)].reshape(m_half, d)
        dtp[i * m_half : (i + 1) * m_half, 0:nh] = lax.dot_general(
            lhs, w_dt[...], (((1,), (1,)), ((), ())), preferred_element_type=F32
        )
    edge = push(pre.at[pl.ds(toks, 8)], pre.at[pl.ds(0, 8)], nxt)

    step_all = jax.nn.softplus(dtp[...] + prm[0:1, :])
    dtp[...] = step_all
    rate = step_all * prm[1:2, :]
    ti = lax.broadcasted_iota(jnp.int32, (BLOCK, BLOCK), 0)
    si = lax.broadcasted_iota(jnp.int32, (BLOCK, BLOCK), 1)
    tri = jnp.where(ti >= si, 1.0, 0.0)
    for b in range(n_blocks):
        ldb[b] = jnp.dot(
            tri,
            rate[b * BLOCK : (b + 1) * BLOCK],
            precision=lax.Precision.HIGHEST,
            preferred_element_type=F32,
        )

    edge.wait_recv()
    for r in range(toks // 64):
        r0 = r * 64
        own = idc[8 + r0 : 72 + r0, :][:, 0:1]
        run_x = jnp.broadcast_to(bias_x[...], (64, el))
        run_bc = jnp.broadcast_to(bias_bc[...], (64, 256))
        for k in range(4):
            at = r0 + 5 + k
            keep = jnp.where(idc[at : at + 64, :][:, 0:1] == own, 1.0, 0.0)
            run_x = run_x + keep * conv_x[k : k + 1, :] * pre[at : at + 64, 0:el]
            run_bc = run_bc + keep * conv_bc[k : k + 1, :] * pre[at : at + 64, el : el + 256]
        xc[r0 : r0 + 64, :] = jax.nn.silu(run_x)
        bcm[r0 : r0 + 64, :] = jax.nn.silu(run_bc).astype(BF16)

    keeps = []
    for b in range(n_blocks):
        r0 = b * BLOCK
        ld = ldb[b]
        ld_end = ld[BLOCK - 1 : BLOCK, :]
        seg = idc[8 + r0 : 8 + r0 + BLOCK, :]
        seg_end = seg[BLOCK - 1 : BLOCK, :]
        prev = idc[7 + r0 : 8 + r0, :]
        step_b = dtp[r0 : r0 + BLOCK, :]
        to_end = jnp.exp(ld_end - ld) * jnp.where(seg == seg_end, 1.0, 0.0) * step_b
        x_b = xc[r0 : r0 + BLOCK, :]
        xp[r0 : r0 + BLOCK, :] = (x_b * lanes_of(step_b, spread)).astype(BF16)
        x_w = (x_b * lanes_of(to_end, spread)).astype(BF16)
        st[b] = lax.dot_general(
            bcm[r0 : r0 + BLOCK, 0:128],
            x_w,
            (((0,), (0,)), ((), ())),
            preferred_element_type=F32,
        )
        keep = jnp.exp(ld_end) * jnp.where(seg_end == prev, 1.0, 0.0)
        keeps.append(jnp.broadcast_to(keep, (8, 128)))
    keep_lanes = [lanes_of(k, spread)[0:1, :] for k in keeps]
    total = st[0]
    keep_shard = keeps[0]
    for b in range(1, n_blocks):
        total = keep_lanes[b] * total + st[b]
        keep_shard = keep_shard * keeps[b]
    a_out[...] = total.reshape(n_seq, ng, el).astype(BF16)
    k_out[...] = keep_shard

    project(w_zx, 0, el, gate, 0, 0)

    state_copies, keep_copies = [], []
    for k in range(1, n_seq):
        peer = lax.rem(seq + k, n_seq)
        where = {"seq": peer}
        keep_copies.append(push(k_out, k_in.at[seq], where))
        state_copies.append(push(a_out.at[peer], a_in.at[seq], where))
    a_in[seq] = a_out[seq]
    k_in[seq] = k_out[...]

    for b in range(n_blocks):
        r0 = b * BLOCK
        ld = ldb[b]
        ld_t = ld.T
        seg = idc[8 + r0 : 8 + r0 + BLOCK, :]
        seg_t = seg.T
        same = seg[:, 0:1] == seg_t[0:1, :]
        gram = lax.dot_general(
            bcm[r0 : r0 + BLOCK, 128:256],
            bcm[r0 : r0 + BLOCK, 0:128],
            (((1,), (1,)), ((), ())),
            preferred_element_type=F32,
        )
        gram = jnp.where(same & (ti >= si), gram, 0.0)
        for pair in range(nh // 2):
            cols = slice(pair * 128, pair * 128 + 128)
            x_pair = xp[r0 : r0 + BLOCK, cols]
            outs = []
            for j in range(2):
                hh = pair * 2 + j
                a = ld[:, hh : hh + 1]
                bb = ld_t[hh : hh + 1, :]
                w0 = jnp.exp(jnp.minimum(a[0:128] - bb[:, 0:128], 0.0)) * gram[0:128, 0:128]
                w1 = jnp.exp(jnp.minimum(a[128:] - bb, 0.0)) * gram[128:, :]
                outs.append(
                    (
                        jnp.dot(w0.astype(BF16), x_pair[0:128], preferred_element_type=F32),
                        jnp.dot(w1.astype(BF16), x_pair, preferred_element_type=F32),
                    )
                )
            first = lax.broadcasted_iota(jnp.int32, (128, 128), 1) < 64
            acc[r0 : r0 + 128, cols] = jnp.where(first, outs[0][0], outs[1][0])
            acc[r0 + 128 : r0 + 256, cols] = jnp.where(first, outs[0][1], outs[1][1])

        if b == 0:
            for copy in keep_copies + state_copies:
                copy.wait_recv()
            decay = lanes_of(k_in[...].reshape(n_seq * 8, 128), spread)
            run = jnp.zeros((ng, el), F32)
            for s in range(n_seq):
                i_out[s] = run.astype(BF16)
                run = decay[s * 8 : s * 8 + 1, :] * run + a_in[s].astype(F32)
            back_copies = []
            for k in range(1, n_seq):
                peer = lax.rem(seq + k, n_seq)
                back_copies.append(push(i_out.at[peer], i_in.at[seq], {"seq": peer}))
            i_in[seq] = i_out[seq]

    loads[3].wait()
    for copy in back_copies:
        copy.wait_recv()

    state = i_in[...].astype(F32).reshape(128, el)
    skip = lanes_of(jnp.broadcast_to(prm[2:3, :], (8, 128)), spread)[0:1, :]
    for b in range(n_blocks):
        r0 = b * BLOCK
        seg = idc[8 + r0 : 8 + r0 + BLOCK, :]
        prev = idc[7 + r0 : 8 + r0, :]
        reach = lanes_of(jnp.exp(ldb[b]) * jnp.where(seg == prev, 1.0, 0.0), spread)
        inter = jnp.dot(
            bcm[r0 : r0 + BLOCK, 128:256], state.astype(BF16), preferred_element_type=F32
        )
        out = acc[r0 : r0 + BLOCK, :] + reach * inter + skip * xc[r0 : r0 + BLOCK, :]
        gated = out * jax.nn.silu(gate[r0 : r0 + BLOCK, :])
        sq = jnp.sum(gated * gated, axis=1, keepdims=True)
        xp[r0 : r0 + BLOCK, :] = (gated * gated_gain[...]).astype(BF16)
        for q in range(2):
            col = jnp.broadcast_to(sq[q * 128 : q * 128 + 128], (128, 128))
            sq_out[b * 2 + q] = col.T[0:8, :]
        state = keep_lanes[b] * state + st[b]

    def out_rows(yy):
        lhs = xp[pl.ds(pl.multiple_of(yy * 2 * rows, 2 * rows), 2 * rows), :]
        wide = 512 if d % 512 == 0 else 256

        def step(i, carry):
            cols = pl.ds(pl.multiple_of(i * wide, wide), wide)
            part[yy, :, cols] = jnp.dot(
                lhs, w_out[:, cols], preferred_element_type=F32
            ).astype(BF16)
            return carry

        lax.fori_loop(0, d // wide, step, 0)

    def mine(xx):
        return pl.ds(pl.multiple_of(xx * rows, rows), rows)

    out_rows(far)
    sq_copies = []
    for k in range(1, n_tp):
        peer = lax.rem(tp + k, n_tp)
        sq_copies.append(push(sq_out.at[peer // 2], sq_in.at[tp], {"tp": peer}))
    sq_in[tp] = sq_out[y]
    out_rows(up)
    r2u = push(part.at[far, pl.ds(0, rows), right], yr2.at[0], at_up)
    r2d = push(part.at[far, pl.ds(rows, rows), right], yr2.at[1], at_down)
    l_far = push(part.at[far, mine(other), left], xl_in.at[far], at_x)
    out_rows(down)
    r3u = push(part.at[up, pl.ds(rows, rows), right], yr1.at[0, 1], at_up)
    l_up = push(part.at[up, mine(other), left], xl_in.at[up], at_x)
    out_rows(y)
    r3d = push(part.at[down, pl.ds(0, rows), right], yr1.at[1, 0], at_down)
    l_down = push(part.at[down, mine(other), left], xl_in.at[down], at_x)
    l_own = push(part.at[y, mine(other), left], xl_in.at[y], at_x)

    l_far.wait_recv()
    ql[far] = (
        part[far, mine(xl), left].astype(F32) + xl_in[far].astype(F32)
    ).astype(BF16)
    r2u.wait_recv()
    qr[0] = (part[up, pl.ds(0, rows), right].astype(F32) + yr2[0].astype(F32)).astype(BF16)
    l2u = push(ql.at[far, pl.ds(0, half)], yl2.at[0], at_up)
    l2d = push(ql.at[far, pl.ds(half, half)], yl2.at[1], at_down)
    r2d.wait_recv()
    qr[1] = (part[down, pl.ds(rows, rows), right].astype(F32) + yr2[1].astype(F32)).astype(BF16)
    r4u = push(qr.at[0], yr1.at[0, 0], at_up)
    l_up.wait_recv()
    ql[up] = (part[up, mine(xl), left].astype(F32) + xl_in[up].astype(F32)).astype(BF16)
    r4d = push(qr.at[1], yr1.at[1, 1], at_down)
    l_down.wait_recv()
    ql[down] = (part[down, mine(xl), left].astype(F32) + xl_in[down].astype(F32)).astype(BF16)
    l2u.wait_recv()
    ql[up, pl.ds(0, half), :] = (
        ql[up, pl.ds(0, half), :].astype(F32) + yl2[0].astype(F32)
    ).astype(BF16)
    l2d.wait_recv()
    ql[down, pl.ds(half, half), :] = (
        ql[down, pl.ds(half, half), :].astype(F32) + yl2[1].astype(F32)
    ).astype(BF16)
    l3u = push(ql.at[up], yl1.at[0], at_up)
    l3d = push(ql.at[down], yl1.at[1], at_down)
    for copy in (r3u, r3d, r4u, r4d):
        copy.wait_recv()

    def right_sum(xx):
        return (
            part[y, mine(xx), right].astype(F32)
            + yr1[0, xx].astype(F32)
            + yr1[1, xx].astype(F32)
        )

    qx[...] = right_sum(other).astype(BF16)

    for copy in sq_copies:
        copy.wait_recv()
    x6 = push(qx, xr_in, at_x)
    tot = sq_in[0]
    for k in range(1, n_tp):
        tot = tot + sq_in[k]
    sqc[...] = jnp.broadcast_to(tot[0:1, :], (128, 128)).T
    factor = lax.rsqrt(sqc[mine(xl), :][:, 0:1] / (el * n_tp) + EPS)

    l_own.wait_recv()
    l3u.wait_recv()
    l3d.wait_recv()
    own_l = (
        part[y, mine(xl), left].astype(F32)
        + xl_in[y].astype(F32)
        + yl1[0].astype(F32)
        + yl1[1].astype(F32)
    )
    result[:, left] = (hid[:, left].astype(F32) + factor * own_l).astype(BF16)
    mine_r = right_sum(xl)
    x6.wait_recv()
    own_r = mine_r + xr_in[...].astype(F32)
    result[:, right] = (hid[:, right].astype(F32) + factor * own_r).astype(BF16)

    for copy in sent:
        copy.wait_send()

    @pl.when(pipe == 0)
    def _():
        handoff.start()
        handoff.wait_send()


def local(geo, *args):
    n_seq, n_tp, n_y, d, el, nh, cl = geo
    (
        hidden_in,
        doc_ids,
        norm_gain,
        in_zx,
        in_bc,
        in_dt,
        conv_x,
        conv_bc,
        bias_x,
        bias_bc,
        dt_bias,
        a_log,
        d_skip,
        gated_gain,
        out_w,
    ) = args
    rows = hidden_in.shape[1]
    toks = rows * n_tp
    ng = 128 // n_seq
    cr = d - cl
    n_blocks = toks // BLOCK
    n_msg = 19 + 3 * (n_seq - 1) + (n_tp - 1) + 15
    vmem = pl.BlockSpec(memory_space=pltpu.VMEM)
    anyw = pl.BlockSpec(memory_space=pl.ANY)
    scratch = [
        pltpu.VMEM((d, 2 * el), BF16),
        pltpu.VMEM((d, 256), BF16),
        pltpu.VMEM((nh, d), BF16),
        pltpu.VMEM((el, d), BF16),
        pltpu.VMEM((rows, d), BF16),
        pltpu.VMEM((n_tp, rows, d), BF16),
        pltpu.VMEM((toks + 8, el + 256), F32),
        pltpu.VMEM((toks, el), F32),
        pltpu.VMEM((toks, el), F32),
        pltpu.VMEM((toks, 256), BF16),
        pltpu.VMEM((toks, el), BF16),
        pltpu.VMEM((toks, el), F32),
        pltpu.VMEM((toks + 8, 128), F32),
        pltpu.VMEM((toks, 128), F32),
        pltpu.VMEM((8, 128), F32),
        pltpu.VMEM((n_blocks, BLOCK, 128), F32),
        pltpu.VMEM((n_blocks, 128, el), F32),
        pltpu.VMEM((n_seq, ng, el), BF16),
        pltpu.VMEM((n_seq, ng, el), BF16),
        pltpu.VMEM((8, 128), F32),
        pltpu.VMEM((n_seq, 8, 128), F32),
        pltpu.VMEM((n_seq, ng, el), BF16),
        pltpu.VMEM((n_seq, ng, el), BF16),
        pltpu.VMEM((n_y, 2 * rows, d), BF16),
        pltpu.VMEM((n_y, rows, cl), BF16),
        pltpu.VMEM((n_y, rows, cl), BF16),
        pltpu.VMEM((2, rows // 2, cl), BF16),
        pltpu.VMEM((2, rows, cl), BF16),
        pltpu.VMEM((2, rows, cr), BF16),
        pltpu.VMEM((2, 2, rows, cr), BF16),
        pltpu.VMEM((2, rows, cr), BF16),
        pltpu.VMEM((rows, cr), BF16),
        pltpu.VMEM((rows, cr), BF16),
        pltpu.VMEM((n_y, 8, 128), F32),
        pltpu.VMEM((n_tp, 8, 128), F32),
        pltpu.VMEM((128, 128), F32),
        pltpu.SemaphoreType.DMA((n_msg,)),
        pltpu.SemaphoreType.DMA((n_msg,)),
        pltpu.SemaphoreType.DMA((5,)),
    ]
    out = pl.pallas_call(
        functools.partial(layer_kernel, geo),
        out_shape=jax.ShapeDtypeStruct((rows, d), BF16),
        in_specs=[anyw, vmem, vmem, anyw, anyw, anyw] + [vmem] * 8 + [anyw],
        out_specs=vmem,
        scratch_shapes=scratch,
        name="mixer_section",
        compiler_params=pltpu.CompilerParams(
            collective_id=0, has_side_effects=True, vmem_limit_bytes=60 * 1024 * 1024
        ),
    )(
        hidden_in[0],
        doc_ids,
        norm_gain,
        in_zx[0].reshape(d, 2 * el),
        in_bc[0],
        in_dt[0].T,
        conv_x[0],
        conv_bc[0],
        bias_x,
        bias_bc,
        dt_bias,
        a_log,
        d_skip,
        gated_gain,
        out_w[0],
    )
    return out[None, None]


def build(mesh, d, e, h):
    n_seq, n_tp = mesh.shape["seq"], mesh.shape["tp"]
    cl = max(128, (d * 9 // 20) // 128 * 128)
    geo = (n_seq, n_tp, n_tp // 2, d, e // n_tp, h // n_tp, cl)
    in_specs = (
        P(None, ("seq", "tp"), None),
        P(None, "seq"),
        P("pipe", None),
        P("pipe", None, None, "tp"),
        P("pipe", None, None),
        P("pipe", None, "tp"),
        P("pipe", None, "tp"),
        P("pipe", None, None),
        P("pipe", "tp"),
        P("pipe", None),
        P("pipe", "tp"),
        P("pipe", "tp"),
        P("pipe", "tp"),
        P("pipe", "tp"),
        P("pipe", "tp", None),
    )
    out_specs = P("pipe", None, ("seq", "tp"), None)
    return jax.shard_map(
        functools.partial(local, geo),
        mesh=mesh,
        in_specs=in_specs,
        out_specs=out_specs,
        check_vma=False,
    )


def solution(mesh):
    return build(mesh, 2560, 5120, 80)
```

time: 466 us -> 142 us (0.30)
  waiting for transfers between devices: 171 us -> 0 us
  Pallas kernels: 0 us -> 133 us
  blocking collectives: 103 us -> 0 us
  matrix products: 68.5 us -> 0 us
  other arithmetic: 39.8 us -> 0 us
  starting transfers between devices: 28.3 us -> 0 us
  local copies, waits for them, and re-layouts: 35 us -> 8.43 us
  between operations: 18.7 us -> 0.01 us
    pallas_call x0 -> x1, Pallas kernels: none -> 133 us  [local(): pl.pallas_call(functools.partial(layer_kernel, geo), out_shape=jax.ShapeD...]
    reduce_scatter x4 -> x0, waiting for transfers between devices: 122 us -> none  [sum_by_axis(): running = lax.psum_scatter(running, axis, scatter_dimension=0, tiled=True)]
    dot_general x26 -> x0, matrix products: 68.5 us -> none  [the longest x2 15.4 us: project_rows(): jnp.dot(normed, weight_zx, preferred_element_type=jnp.float32)]
    all_to_all x2 -> x0, blocking collectives: 45.8 us -> none  [from_everyone(): return lax.all_to_all(copies, axis, split_axis=0, concat_axis=0, tiled=True)]
    unnamed x4 -> x0, blocking collectives: 40.7 us -> none
    all_gather x2 -> x0, waiting for transfers between devices: 33 us -> none  [prefix_by_axis(): pieces = jax.tree.map(lambda part: lax.all_gather(part, axis), running)]
    ppermute x4 -> x0, starting transfers between devices: 17 us -> none  [shifted(): return lax.ppermute(block, axis, route)]
    all_gather x2 -> x0, blocking collectives: 16.9 us -> none  [prefix_by_axis(): pieces = jax.tree.map(lambda part: lax.all_gather(part, axis), running)]
  transfers between devices with their start and end apart: 12 -> 0, of which waited for: 9 -> 0; matrix products, arithmetic and copies ran while one was open for 10% -> 0% of each run, Pallas kernels for 0% -> 0%
where the time goes in v1:
time: 142 us
  Pallas kernels  133 us (94%)
  local copies, waits for them, and re-layouts  8.43 us (6%)
    pallas_call x1, Pallas kernels, local(): pl.pallas_call(functools.partial(layer_kernel, geo), out_shape=jax.ShapeD...  133 us
    unnamed x2, local copies, waits for them, and re-layouts  8.43 us

profile of v1, /device:TPU:1, one launch (start us, length us, event | category | flops | bytes accessed | tf_op | source)
XLA Modules:
  0.0 141.8 jit_solution(1181526924579426857)
XLA Ops:
  0.0 6.7 %copy.16 = bf16[320,8,2,640]{3,1,2,0:T(8,128)(2,1)} copy(bf16[320,8,2,640]{3,2,1,0:T(2,128)(2,1)} %bitcast.13) | data formatting | bytes 13107200
  6.7 133.3 %mixer_section.1 = bf16[64,2560]{1,0:T(8,128)(2,1)} custom-call(bf16[64,2560]{1,0:T(8,128)(2,1)} %bitcast.17, s32[1,512]{1,0:T(1,128)} %ids_ref.1, f32[1,2560]{1,0:T(1,128)} %norm_gain.1, bf16[2560,1280]{1,0:T(8,128)(2,1)} %bitcast.12, bf16[2560,256]{1,0:T(8,128)(2,1)} %bitcast.16, bf16[10,2560]{1,0:T(8,128)(2,1)} %bitcast.18, f32[4,640]{1,0:T(4,128)} %bitcast.19, ...), custom_call_target="tpu_custom_call" | custom-call | tf_op jit(solution)/shard_map/mixer_section/pallas_call | solution.py:553
  140.1 1.7 %copy.18 = bf16[1,1,64,2560]{3,2,1,0:T(8,128)(2,1)} copy(bf16[1,1,64,2560]{3,2,1,0:T(8,128)(2,1)} %bitcast.15) | data formatting | bytes 655360

commit v2 on v1

v2 whole, which is shorter than its diff:
```python
import functools

import jax
import jax.numpy as jnp
from jax import lax
from jax.experimental import pallas as pl
from jax.experimental.pallas import tpu as pltpu
from jax.sharding import PartitionSpec as P

BLOCK = 256
EPS = 1e-05
F32 = jnp.float32
BF16 = jnp.bfloat16
MESH = pl.DeviceIdType.MESH


def lanes_of(v, spread):
    hi = v.astype(BF16)
    lo = (v - hi.astype(F32)).astype(BF16)
    return jnp.dot(hi, spread, preferred_element_type=F32) + jnp.dot(
        lo, spread, preferred_element_type=F32
    )


def layer_kernel(
    geo,
    hidden_hbm,
    ids_ref,
    norm_gain,
    zx_hbm,
    bc_hbm,
    dt_hbm,
    conv_x,
    conv_bc,
    bias_x,
    bias_bc,
    dt_bias,
    a_log,
    d_skip,
    gated_gain,
    out_hbm,
    result,
    w_raw,
    w_gate,
    w_x,
    w_bc,
    w_dt,
    w_out,
    hid,
    rows_all,
    pre,
    gate,
    xc,
    bcm,
    xp,
    acc,
    idc,
    dtp,
    prm,
    ldb,
    st,
    grams,
    a_out,
    a_in,
    i_out,
    i_in,
    part,
    xl_in,
    ql,
    yl2,
    yl1,
    yr2,
    yr1,
    qr,
    qx,
    xr_in,
    sq_out,
    sq_in,
    sqc,
    send_sem,
    recv_sem,
    load_sem,
):
    n_seq, n_tp, n_y, d, el, nh, pieces = geo
    pipe, seq, tp = lax.axis_index("pipe"), lax.axis_index("seq"), lax.axis_index("tp")
    y, xl = tp // 2, tp % 2
    other = 1 - xl
    rows = hid.shape[0]
    toks = n_tp * rows
    half = rows // 2
    n_blocks = toks // BLOCK
    ng = 128 // n_seq
    up, down = lax.rem(y + 1, n_y), lax.rem(y + n_y - 1, n_y)
    far = lax.rem(y + 2, n_y)
    at_up = {"tp": up * 2 + xl}
    at_down = {"tp": down * 2 + xl}
    at_x = {"tp": y * 2 + other}
    nxt = {"seq": lax.rem(seq + 1, n_seq)}
    every = range(len(pieces))
    rights = [i for i in every if pieces[i][2]]
    lefts = [i for i in every if not pieces[i][2]]
    cols = [pl.ds(c0, w) for c0, w, _ in pieces]
    counter = [0]
    sent = []

    def remote(src, dst, where):
        k = counter[0]
        counter[0] += 1
        return pltpu.make_async_remote_copy(
            src_ref=src,
            dst_ref=dst,
            send_sem=send_sem.at[k],
            recv_sem=recv_sem.at[k],
            device_id=where,
            device_id_type=MESH,
        )

    def push(src, dst, where):
        copy = remote(src, dst, where)
        copy.start()
        sent.append(copy)
        return copy

    loads = [
        pltpu.make_async_copy(s, t, load_sem.at[k])
        for k, (s, t) in enumerate(
            [(zx_hbm, w_raw), (dt_hbm, w_dt), (bc_hbm, w_bc), (out_hbm, w_out)]
        )
    ]
    first_load = pltpu.make_async_copy(hidden_hbm, hid, load_sem.at[4])

    @pl.when(pipe == 0)
    def _():
        first_load.start()

    for copy in loads:
        copy.start()

    barrier = pltpu.get_barrier_semaphore()
    for k in range(1, n_seq):
        pl.semaphore_signal(
            barrier, inc=1, device_id={"seq": lax.rem(seq + k, n_seq)}, device_id_type=MESH
        )
    for k in range(1, n_tp):
        pl.semaphore_signal(
            barrier, inc=1, device_id={"tp": lax.rem(tp + k, n_tp)}, device_id_type=MESH
        )
    pl.semaphore_signal(barrier, inc=1, device_id={"pipe": 1 - pipe}, device_id_type=MESH)

    prm[...] = jnp.zeros_like(prm)
    prm[0:1, 0:nh] = dt_bias[...]
    prm[1:2, 0:nh] = -jnp.exp(a_log[...])
    prm[2:3, 0:nh] = d_skip[...]
    ids_row = ids_ref[...].astype(F32)
    idc[8 : 8 + toks, :] = jnp.broadcast_to(ids_row, (128, toks)).T
    head = lax.broadcasted_iota(jnp.int32, (128, el), 0)
    lane = lax.broadcasted_iota(jnp.int32, (128, el), 1)
    spread = jnp.where((lane // 64) == head, 1.0, 0.0).astype(BF16)
    ti = lax.broadcasted_iota(jnp.int32, (BLOCK, BLOCK), 0)
    si = lax.broadcasted_iota(jnp.int32, (BLOCK, BLOCK), 1)

    def lay_out(lo, hi):
        def step(i, carry):
            r = pl.multiple_of(i * 64, 64)
            both = jnp.swapaxes(w_raw[pl.ds(r, 64)].astype(F32), 0, 1)
            w_gate[pl.ds(r, 64), :] = both[0].astype(BF16)
            w_x[pl.ds(r, 64), 0:el] = both[1].astype(BF16)
            return carry

        lax.fori_loop(lo, hi, step, 0)

    def lay_out_dt():
        unit = jnp.where(
            lax.broadcasted_iota(jnp.int32, (nh, 128), 0)
            == lax.broadcasted_iota(jnp.int32, (nh, 128), 1),
            1.0,
            0.0,
        ).astype(BF16)
        for r in range(0, d, 256):
            w_x[r : r + 256, el : el + 128] = lax.dot_general(
                w_dt[:, r : r + 256],
                unit,
                (((0,), (0,)), ((), ())),
                preferred_element_type=F32,
            ).astype(BF16)

    n_lay = d // 64
    loads[1].wait()
    lay_out_dt()

    pl.semaphore_wait(barrier, n_tp + n_seq - 1)
    id_edge = push(idc.at[pl.ds(toks, 8)], idc.at[pl.ds(0, 8)], nxt)
    handoff = [remote(result.at[:, c], hid.at[:, c], {"pipe": 1 - pipe}) for c in cols]

    @pl.when(pipe == 0)
    def _():
        first_load.wait()

    loads[0].wait()

    @pl.when(pipe == 1)
    def _():
        lay_out(0, n_lay)
        for copy in handoff:
            copy.wait_recv()

    h = hid[...].astype(F32)
    scale = lax.rsqrt(jnp.mean(h * h, axis=1, keepdims=True) + EPS)
    rows_all[tp] = (h * scale * norm_gain[...]).astype(BF16)

    def hop(yy, xx, i, where, r0=0, n=rows):
        s = rows_all.at[yy * 2 + xx, pl.ds(r0, n), cols[i]]
        return push(s, s, where)

    u1, d1, x1 = {}, {}, {}
    for i in every:
        u1[i], d1[i] = hop(y, xl, i, at_up), hop(y, xl, i, at_down)
        x1[i] = hop(y, xl, i, at_x)

    @pl.when(pipe == 0)
    def _():
        lay_out(0, n_lay // 2)

    u2, d2, x2, x3 = {}, {}, {}, {}
    for i in every:
        if i in rights:
            x1[i].wait_recv()
            u2[i], d2[i] = hop(y, other, i, at_up), hop(y, other, i, at_down)
        else:
            u1[i].wait_recv()
            u2[i] = hop(down, xl, i, at_up, 0, half)
            x2[i] = hop(down, xl, i, at_x)
            d1[i].wait_recv()
            d2[i] = hop(up, xl, i, at_down, half, half)
            x3[i] = hop(up, xl, i, at_x)

    @pl.when(pipe == 0)
    def _():
        lay_out(n_lay // 2, n_lay)

    u3, d3, x4 = {}, {}, {}
    for i in every:
        if i in rights:
            u1[i].wait_recv()
            u2[i].wait_recv()
            u3[i] = hop(down, 0, i, at_up)
            d1[i].wait_recv()
            d2[i].wait_recv()
            d3[i] = hop(up, 1, i, at_down)
        else:
            u2[i].wait_recv()
            d2[i].wait_recv()
            x4[i] = hop(far, xl, i, at_x)

    id_edge.wait_recv()
    idc[0:8, :] = jnp.where(seq > 0, idc[0:8, :], -1.0)
    loads[2].wait()
    n_half = n_tp // 2
    m_half = n_half * rows

    def project(weight, w0, w, target, t0, r0, i):
        for j in range(2):
            lhs = rows_all[n_half * j : n_half * (j + 1), :, cols[i]].reshape(
                m_half, pieces[i][1]
            )
            at = (pl.ds(r0 + j * m_half, m_half), pl.ds(t0, w))
            term = jnp.dot(lhs, weight[cols[i], pl.ds(w0, w)], preferred_element_type=F32)
            target[at] = term if i == 0 else target[at] + term

    for i in every:
        if i in rights:
            u3[i].wait_recv()
            d3[i].wait_recv()
        else:
            for copy in (x1[i], x2[i], x3[i], x4[i]):
                copy.wait_recv()

        def step(t, carry, i=i):
            c0 = pl.multiple_of(t * 256, 256)
            project(w_x, c0, 256, pre, c0, 8, i)
            return carry

        lax.fori_loop(0, (el + 128) // 256, step, 0)
        project(w_bc, 0, 256, pre, el + 128, 8, i)

    step_all = jax.nn.softplus(pre[8 : 8 + toks, el : el + 128] + prm[0:1, :])
    dtp[...] = step_all
    edge = push(pre.at[pl.ds(toks, 8)], pre.at[pl.ds(0, 8)], nxt)
    rate = step_all * prm[1:2, :]
    tri = jnp.where(ti >= si, 1.0, 0.0)
    for b in range(n_blocks):
        ldb[b] = jnp.dot(
            tri,
            rate[b * BLOCK : (b + 1) * BLOCK],
            precision=lax.Precision.HIGHEST,
            preferred_element_type=F32,
        )

    def convolve(r):
        r0 = r * 64
        own = idc[8 + r0 : 72 + r0, :][:, 0:1]
        run_x = jnp.broadcast_to(bias_x[...], (64, el))
        run_bc = jnp.broadcast_to(bias_bc[...], (64, 256))
        for k in range(4):
            at = r0 + 5 + k
            keep = jnp.where(idc[at : at + 64, :][:, 0:1] == own, 1.0, 0.0)
            run_x = run_x + keep * conv_x[k : k + 1, :] * pre[at : at + 64, 0:el]
            run_bc = run_bc + keep * conv_bc[k : k + 1, :] * pre[at : at + 64, el + 128 :]
        xc[r0 : r0 + 64, :] = jax.nn.silu(run_x)
        bcm[r0 : r0 + 64, :] = jax.nn.silu(run_bc).astype(BF16)

    for r in range(1, toks // 64):
        convolve(r)

    def project_gate(c0, w):
        for j in range(2):
            lhs = rows_all[n_half * j : n_half * (j + 1)].reshape(m_half, d)
            gate[pl.ds(j * m_half, m_half), pl.ds(c0, w)] = jnp.dot(
                lhs, w_gate[:, pl.ds(c0, w)], preferred_element_type=F32
            )

    gate_tiles = [(c0, min(256, el - c0)) for c0 in range(0, el, 256)]
    for tile in gate_tiles[:-1]:
        project_gate(*tile)

    edge.wait_recv()
    convolve(0)

    keeps = []
    for b in range(n_blocks):
        r0 = b * BLOCK
        ld = ldb[b]
        ld_end = ld[BLOCK - 1 : BLOCK, :]
        seg = idc[8 + r0 : 8 + r0 + BLOCK, :]
        seg_end = seg[BLOCK - 1 : BLOCK, :]
        prev = idc[7 + r0 : 8 + r0, :]
        step_b = dtp[r0 : r0 + BLOCK, :]
        to_end = jnp.exp(ld_end - ld) * jnp.where(seg == seg_end, 1.0, 0.0) * step_b
        x_b = xc[r0 : r0 + BLOCK, :]
        x_w = (x_b * lanes_of(to_end, spread)).astype(BF16)
        st[b] = lax.dot_general(
            bcm[r0 : r0 + BLOCK, 0:128],
            x_w,
            (((0,), (0,)), ((), ())),
            preferred_element_type=F32,
        )
        keep = jnp.exp(ld_end) * jnp.where(seg_end == prev, 1.0, 0.0)
        keeps.append(jnp.broadcast_to(keep, (8, 128)))
    keep_lanes = [lanes_of(k, spread)[0:1, :] for k in keeps]
    total = st[0]
    keep_shard = keeps[0]
    for b in range(1, n_blocks):
        total = keep_lanes[b] * total + st[b]
        keep_shard = keep_shard * keeps[b]
    a_out[:, :, 0:el] = total.reshape(n_seq, ng, el).astype(BF16)
    keep_row = jnp.broadcast_to(keep_shard[0:1, :], (ng, 128))
    k_hi = keep_row.astype(BF16).astype(F32)
    k_mid = (keep_row - k_hi).astype(BF16).astype(F32)
    k_lo = keep_row - k_hi - k_mid
    which = lax.broadcasted_iota(jnp.int32, (ng, 128), 0)
    k_rows = jnp.where(
        which == 0, k_hi, jnp.where(which == 1, k_mid, jnp.where(which == 2, k_lo, 0.0))
    ).astype(BF16)
    for s in range(n_seq):
        a_out[s, :, el : el + 128] = k_rows

    for b in range(n_blocks):
        r0 = b * BLOCK
        seg = idc[8 + r0 : 8 + r0 + BLOCK, :]
        same = seg[:, 0:1] == seg.T[0:1, :]
        gram = lax.dot_general(
            bcm[r0 : r0 + BLOCK, 128:256],
            bcm[r0 : r0 + BLOCK, 0:128],
            (((1,), (1,)), ((), ())),
            preferred_element_type=F32,
        )
        grams[b] = jnp.where(same & (ti >= si), gram, 0.0)

    state_copies = []
    for k in range(1, n_seq):
        peer = lax.rem(seq + k, n_seq)
        state_copies.append(push(a_out.at[peer], a_in.at[seq], {"seq": peer}))
    a_in[seq] = a_out[seq]
    project_gate(*gate_tiles[-1])
    for b in range(n_blocks):
        r0 = b * BLOCK
        xp[r0 : r0 + BLOCK, :] = (
            xc[r0 : r0 + BLOCK, :] * lanes_of(dtp[r0 : r0 + BLOCK, :], spread)
        ).astype(BF16)

    def inside(b):
        r0 = b * BLOCK
        ld = ldb[b]
        ld_t = ld.T
        gram = grams[b]
        for pair in range(nh // 2):
            cs = slice(pair * 128, pair * 128 + 128)
            x_pair = xp[r0 : r0 + BLOCK, cs]
            outs = []
            for j in range(2):
                hh = pair * 2 + j
                a = ld[:, hh : hh + 1]
                bb = ld_t[hh : hh + 1, :]
                w0 = jnp.exp(jnp.minimum(a[0:128] - bb[:, 0:128], 0.0)) * gram[0:128, 0:128]
                w1 = jnp.exp(jnp.minimum(a[128:] - bb, 0.0)) * gram[128:, :]
                outs.append(
                    (
                        jnp.dot(w0.astype(BF16), x_pair[0:128], preferred_element_type=F32),
                        jnp.dot(w1.astype(BF16), x_pair, preferred_element_type=F32),
                    )
                )
            first = lax.broadcasted_iota(jnp.int32, (128, 128), 1) < 64
            acc[r0 : r0 + 128, cs] = jnp.where(first, outs[0][0], outs[1][0])
            acc[r0 + 128 : r0 + 256, cs] = jnp.where(first, outs[0][1], outs[1][1])

    inside(0)

    for copy in state_copies:
        copy.wait_recv()

    decay = jnp.dot(
        a_in[:, :, el : el + 128].reshape(n_seq * ng, 128), spread, preferred_element_type=F32
    )
    run = jnp.zeros((ng, el), F32)
    for s in range(n_seq):
        i_out[s] = run.astype(BF16)
        k0 = s * ng
        keep = decay[k0 : k0 + 1, :] + decay[k0 + 1 : k0 + 2, :] + decay[k0 + 2 : k0 + 3, :]
        run = keep * run + a_in[s, :, 0:el].astype(F32)
    back_copies = []
    for k in range(1, n_seq):
        peer = lax.rem(seq + k, n_seq)
        back_copies.append(push(i_out.at[peer], i_in.at[seq], {"seq": peer}))
    i_in[seq] = i_out[seq]
    for b in range(1, n_blocks):
        inside(b)
    loads[3].wait()

    for copy in back_copies:
        copy.wait_recv()

    state = i_in[...].astype(F32).reshape(128, el)
    skip = lanes_of(jnp.broadcast_to(prm[2:3, :], (8, 128)), spread)[0:1, :]
    for b in range(n_blocks):
        r0 = b * BLOCK
        seg = idc[8 + r0 : 8 + r0 + BLOCK, :]
        prev = idc[7 + r0 : 8 + r0, :]
        reach = lanes_of(jnp.exp(ldb[b]) * jnp.where(seg == prev, 1.0, 0.0), spread)
        inter = jnp.dot(
            bcm[r0 : r0 + BLOCK, 128:256], state.astype(BF16), preferred_element_type=F32
        )
        out = acc[r0 : r0 + BLOCK, :] + reach * inter + skip * xc[r0 : r0 + BLOCK, :]
        gated = out * jax.nn.silu(gate[r0 : r0 + BLOCK, :])
        sq = jnp.sum(gated * gated, axis=1, keepdims=True)
        xp[r0 : r0 + BLOCK, :] = (gated * gated_gain[...]).astype(BF16)
        for q in range(2):
            col = jnp.broadcast_to(sq[q * 128 : q * 128 + 128], (128, 128))
            sq_out[b * 2 + q] = col.T[0:8, :]
        state = keep_lanes[b] * state + st[b]

    def out_cols(i):
        for q in range(2):
            term = jnp.dot(
                xp[q * m_half : (q + 1) * m_half, :],
                w_out[:, cols[i]],
                preferred_element_type=F32,
            ).astype(BF16)
            part[q * (n_y // 2) : (q + 1) * (n_y // 2), :, cols[i]] = term.reshape(
                n_y // 2, 2 * rows, pieces[i][1]
            )

    def mine(xx):
        return pl.ds(pl.multiple_of(xx * rows, rows), rows)

    zero, one = pl.ds(0, rows), pl.ds(rows, rows)
    r2u, r2d, r3u, r3d, r4u, r4d, x6 = {}, {}, {}, {}, {}, {}, {}
    lx = {}
    l2u, l2d, l3u, l3d = {}, {}, {}, {}

    def first_sends(i):
        if i in rights:
            r2u[i] = push(part.at[far, zero, cols[i]], yr2.at[0, :, cols[i]], at_up)
            r2d[i] = push(part.at[far, one, cols[i]], yr2.at[1, :, cols[i]], at_down)
        else:
            lx[i] = [
                push(part.at[yy, mine(other), cols[i]], xl_in.at[yy, :, cols[i]], at_x)
                for yy in (far, up, down, y)
            ]

    def second_sends(i):
        r3u[i] = push(part.at[up, one, cols[i]], yr1.at[0, 1, :, cols[i]], at_up)
        r3d[i] = push(part.at[down, zero, cols[i]], yr1.at[1, 0, :, cols[i]], at_down)

    for i in every:
        out_cols(i)
        if i > 0:
            first_sends(i - 1)
    sq_copies = []
    for k in range(1, n_tp):
        peer = lax.rem(tp + k, n_tp)
        sq_copies.append(push(sq_out.at[peer // 2], sq_in.at[tp], {"tp": peer}))
    sq_in[tp] = sq_out[y]
    first_sends(len(pieces) - 1)
    for i in rights:
        second_sends(i)

    def sum_of(*refs):
        tot = refs[0].astype(F32)
        for r in refs[1:]:
            tot = tot + r.astype(F32)
        return tot

    for i in every:
        c = cols[i]
        if i in rights:
            r2u[i].wait_recv()
            qr[0, :, c] = sum_of(part[up, zero, c], yr2[0, :, c]).astype(BF16)
            r2d[i].wait_recv()
            qr[1, :, c] = sum_of(part[down, one, c], yr2[1, :, c]).astype(BF16)
            r4u[i] = push(qr.at[0, :, c], yr1.at[0, 0, :, c], at_up)
            r4d[i] = push(qr.at[1, :, c], yr1.at[1, 1, :, c], at_down)
        else:
            lx[i][0].wait_recv()
            ql[far, :, c] = sum_of(part[far, mine(xl), c], xl_in[far, :, c]).astype(BF16)
            l2u[i] = push(ql.at[far, pl.ds(0, half), c], yl2.at[0, :, c], at_up)
            l2d[i] = push(ql.at[far, pl.ds(half, half), c], yl2.at[1, :, c], at_down)

    for i in lefts:
        c = cols[i]
        lx[i][1].wait_recv()
        q_up = sum_of(part[up, mine(xl), c], xl_in[up, :, c])
        lx[i][2].wait_recv()
        q_down = sum_of(part[down, mine(xl), c], xl_in[down, :, c])
        l2u[i].wait_recv()
        ql[up, pl.ds(0, half), c] = (q_up[0:half] + yl2[0, :, c].astype(F32)).astype(BF16)
        ql[up, pl.ds(half, half), c] = q_up[half:].astype(BF16)
        l2d[i].wait_recv()
        ql[down, pl.ds(0, half), c] = q_down[0:half].astype(BF16)
        ql[down, pl.ds(half, half), c] = (q_down[half:] + yl2[1, :, c].astype(F32)).astype(BF16)
        l3u[i] = push(ql.at[up, :, c], yl1.at[0, :, c], at_up)
        l3d[i] = push(ql.at[down, :, c], yl1.at[1, :, c], at_down)

    for copy in sq_copies:
        copy.wait_recv()
    tot = sq_in[0]
    for k in range(1, n_tp):
        tot = tot + sq_in[k]
    sqc[...] = jnp.broadcast_to(tot[0:1, :], (128, 128)).T
    factor = lax.rsqrt(sqc[mine(xl), :][:, 0:1] / (el * n_tp) + EPS)

    def right_sum(xx, c):
        return sum_of(part[y, mine(xx), c], yr1[0, xx, :, c], yr1[1, xx, :, c])

    for i in rights:
        c = cols[i]
        for copy in (r3u[i], r3d[i], r4u[i], r4d[i]):
            copy.wait_recv()
        qx[:, c] = right_sum(other, c).astype(BF16)
        x6[i] = push(qx.at[:, c], xr_in.at[:, c], at_x)

    def finish(i, total):
        c = cols[i]
        result[:, c] = (hid[:, c].astype(F32) + factor * total).astype(BF16)

    done = []

    def hand(i):
        done.append(i)

        @pl.when(pipe == 0)
        def _():
            handoff[i].start()

    for i in lefts:
        c = cols[i]
        lx[i][3].wait_recv()
        l3u[i].wait_recv()
        l3d[i].wait_recv()
        finish(i, sum_of(part[y, mine(xl), c], xl_in[y, :, c], yl1[0, :, c], yl1[1, :, c]))
    waiting = list(lefts)
    for i in rights:
        c = cols[i]
        own = right_sum(xl, c)
        x6[i].wait_recv()
        for j in waiting:
            hand(j)
        finish(i, own + xr_in[:, c].astype(F32))
        waiting = [i]
    for j in waiting:
        hand(j)

    for copy in sent:
        copy.wait_send()

    @pl.when(pipe == 0)
    def _():
        for copy in handoff:
            copy.wait_send()


def local(geo, *args):
    n_seq, n_tp, n_y, d, el, nh, pieces = geo
    (
        hidden_in,
        doc_ids,
        norm_gain,
        in_zx,
        in_bc,
        in_dt,
        conv_x,
        conv_bc,
        bias_x,
        bias_bc,
        dt_bias,
        a_log,
        d_skip,
        gated_gain,
        out_w,
    ) = args
    rows = hidden_in.shape[1]
    toks = rows * n_tp
    ng = 128 // n_seq
    n_blocks = toks // BLOCK
    n_right = sum(1 for p in pieces if p[2])
    n_left = len(pieces) - n_right
    n_msg = (
        2 + len(pieces) + 2 * (n_seq - 1) + (n_tp - 1) + 14 * n_right + 16 * n_left
    )
    vmem = pl.BlockSpec(memory_space=pltpu.VMEM)
    anyw = pl.BlockSpec(memory_space=pl.ANY)
    scratch = [
        pltpu.VMEM((d, 2, el), BF16),
        pltpu.VMEM((d, el), BF16),
        pltpu.VMEM((d, el + 128), BF16),
        pltpu.VMEM((d, 256), BF16),
        pltpu.VMEM((nh, d), BF16),
        pltpu.VMEM((el, d), BF16),
        pltpu.VMEM((rows, d), BF16),
        pltpu.VMEM((n_tp, rows, d), BF16),
        pltpu.VMEM((toks + 8, el + 384), F32),
        pltpu.VMEM((toks, el), F32),
        pltpu.VMEM((toks, el), F32),
        pltpu.VMEM((toks, 256), BF16),
        pltpu.VMEM((toks, el), BF16),
        pltpu.VMEM((toks, el), F32),
        pltpu.VMEM((toks + 8, 128), F32),
        pltpu.VMEM((toks, 128), F32),
        pltpu.VMEM((8, 128), F32),
        pltpu.VMEM((n_blocks, BLOCK, 128), F32),
        pltpu.VMEM((n_blocks, 128, el), F32),
        pltpu.VMEM((n_blocks, BLOCK, BLOCK), F32),
        pltpu.VMEM((n_seq, ng, el + 128), BF16),
        pltpu.VMEM((n_seq, ng, el + 128), BF16),
        pltpu.VMEM((n_seq, ng, el), BF16),
        pltpu.VMEM((n_seq, ng, el), BF16),
        pltpu.VMEM((n_y, 2 * rows, d), BF16),
        pltpu.VMEM((n_y, rows, d), BF16),
        pltpu.VMEM((n_y, rows, d), BF16),
        pltpu.VMEM((2, rows // 2, d), BF16),
        pltpu.VMEM((2, rows, d), BF16),
        pltpu.VMEM((2, rows, d), BF16),
        pltpu.VMEM((2, 2, rows, d), BF16),
        pltpu.VMEM((2, rows, d), BF16),
        pltpu.VMEM((rows, d), BF16),
        pltpu.VMEM((rows, d), BF16),
        pltpu.VMEM((n_y, 8, 128), F32),
        pltpu.VMEM((n_tp, 8, 128), F32),
        pltpu.VMEM((128, 128), F32),
        pltpu.SemaphoreType.DMA((n_msg,)),
        pltpu.SemaphoreType.DMA((n_msg,)),
        pltpu.SemaphoreType.DMA((5,)),
    ]
    out = pl.pallas_call(
        functools.partial(layer_kernel, geo),
        out_shape=jax.ShapeDtypeStruct((rows, d), BF16),
        in_specs=[anyw, vmem, vmem, anyw, anyw, anyw] + [vmem] * 8 + [anyw],
        out_specs=vmem,
        scratch_shapes=scratch,
        name="mixer_section",
        compiler_params=pltpu.CompilerParams(
            collective_id=0, has_side_effects=True, vmem_limit_bytes=60 * 1024 * 1024
        ),
    )(
        hidden_in[0],
        doc_ids,
        norm_gain,
        in_zx[0],
        in_bc[0],
        in_dt[0].T,
        conv_x[0],
        conv_bc[0],
        bias_x,
        bias_bc,
        dt_bias,
        a_log,
        d_skip,
        gated_gain,
        out_w[0],
    )
    return out[None, None]


def build(mesh, d, e, h):
    n_seq, n_tp = mesh.shape["seq"], mesh.shape["tp"]
    wide = 512 if d % 512 == 0 else 128
    pieces = tuple((c, wide, (c // wide) % 2 == 0) for c in range(0, d, wide))
    geo = (n_seq, n_tp, n_tp // 2, d, e // n_tp, h // n_tp, pieces)
    in_specs = (
        P(None, ("seq", "tp"), None),
        P(None, "seq"),
        P("pipe", None),
        P("pipe", None, None, "tp"),
        P("pipe", None, None),
        P("pipe", None, "tp"),
        P("pipe", None, "tp"),
        P("pipe", None, None),
        P("pipe", "tp"),
        P("pipe", None),
        P("pipe", "tp"),
        P("pipe", "tp"),
        P("pipe", "tp"),
        P("pipe", "tp"),
        P("pipe", "tp", None),
    )
    out_specs = P("pipe", None, ("seq", "tp"), None)
    return jax.shard_map(
        functools.partial(local, geo),
        mesh=mesh,
        in_specs=in_specs,
        out_specs=out_specs,
        check_vma=False,
    )


def solution(mesh):
    return build(mesh, 2560, 5120, 80)
```

time: 142 us -> 122 us (0.86)
  Pallas kernels: 133 us -> 120 us
  local copies, waits for them, and re-layouts: 8.43 us -> 1.72 us
    pallas_call x1, Pallas kernels: 133 us -> 120 us  [local(): pl.pallas_call(functools.partial(layer_kernel, geo), out_shape=jax.ShapeD...]
    unnamed x2 -> x1, local copies, waits for them, and re-layouts: 8.43 us -> 1.72 us
where the time goes in v2:
time: 122 us
  Pallas kernels  120 us (98%)
  local copies, waits for them, and re-layouts  1.72 us (1%)
    pallas_call x1, Pallas kernels, local(): pl.pallas_call(functools.partial(layer_kernel, geo), out_shape=jax.ShapeD...  120 us

profile of v2, /device:TPU:1, one launch (start us, length us, event | category | flops | bytes accessed | tf_op | source)
XLA Modules:
  0.0 121.8 jit_solution(1925653051883560377)
XLA Ops:
  0.0 120.1 %mixer_section.1 = bf16[64,2560]{1,0:T(8,128)(2,1)} custom-call(bf16[64,2560]{1,0:T(8,128)(2,1)} %bitcast.14, s32[1,512]{1,0:T(1,128)} %ids_ref.1, f32[1,2560]{1,0:T(1,128)} %norm_gain.1, bf16[2560,2,640]{2,1,0:T(2,128)(2,1)} %bitcast.10, bf16[2560,256]{1,0:T(8,128)(2,1)} %bitcast.13, bf16[10,2560]{1,0:T(8,128)(2,1)} %bitcast.15, f32[4,640]{1,0:T(4,128)} %bitcast.16, ...), custom_call_target="tpu_custom_call" | custom-call | tf_op jit(solution)/shard_map/mixer_section/pallas_call | solution.py:673
  120.1 1.7 %copy.17 = bf16[1,1,64,2560]{3,2,1,0:T(8,128)(2,1)} copy(bf16[1,1,64,2560]{3,2,1,0:T(8,128)(2,1)} %bitcast.12) | data formatting | bytes 655360

commit v3 on v2

--- a/solution.py
+++ b/solution.py
@@ -121,13 +121,20 @@
         sent.append(copy)
         return copy
 
-    loads = [
+    top, bottom = pl.ds(0, d // 2), pl.ds(d // 2, d // 2)
+    load_dt, load_top, load_bottom, load_bc, load_out = loads = [
         pltpu.make_async_copy(s, t, load_sem.at[k])
         for k, (s, t) in enumerate(
-            [(zx_hbm, w_raw), (dt_hbm, w_dt), (bc_hbm, w_bc), (out_hbm, w_out)]
+            [
+                (dt_hbm, w_dt),
+                (zx_hbm.at[top], w_raw.at[top]),
+                (zx_hbm.at[bottom], w_raw.at[bottom]),
+                (bc_hbm, w_bc),
+                (out_hbm, w_out),
+            ]
         )
     ]
-    first_load = pltpu.make_async_copy(hidden_hbm, hid, load_sem.at[4])
+    first_load = pltpu.make_async_copy(hidden_hbm, hid, load_sem.at[5])
 
     @pl.when(pipe == 0)
     def _():
@@ -136,8 +143,9 @@
     for copy in loads:
         copy.start()
 
+    far_first = sorted(range(1, n_seq), key=lambda k: abs(2 * k - n_seq))
     barrier = pltpu.get_barrier_semaphore()
-    for k in range(1, n_seq):
+    for k in far_first:
         pl.semaphore_signal(
             barrier, inc=1, device_id={"seq": lax.rem(seq + k, n_seq)}, device_id_type=MESH
         )
@@ -185,8 +193,10 @@
             ).astype(BF16)
 
     n_lay = d // 64
-    loads[1].wait()
+    load_dt.wait()
     lay_out_dt()
+    load_top.wait()
+    lay_out(0, n_lay // 2)
 
     pl.semaphore_wait(barrier, n_tp + n_seq - 1)
     id_edge = push(idc.at[pl.ds(toks, 8)], idc.at[pl.ds(0, 8)], nxt)
@@ -196,11 +206,11 @@
     def _():
         first_load.wait()
 
-    loads[0].wait()
+    load_bottom.wait()
 
     @pl.when(pipe == 1)
     def _():
-        lay_out(0, n_lay)
+        lay_out(n_lay // 2, n_lay)
         for copy in handoff:
             copy.wait_recv()
 
@@ -219,7 +229,7 @@
 
     @pl.when(pipe == 0)
     def _():
-        lay_out(0, n_lay // 2)
+        lay_out(n_lay // 2, n_lay)
 
     u2, d2, x2, x3 = {}, {}, {}, {}
     for i in every:
@@ -234,10 +244,28 @@
             d2[i] = hop(up, xl, i, at_down, half, half)
             x3[i] = hop(up, xl, i, at_x)
 
-    @pl.when(pipe == 0)
-    def _():
-        lay_out(n_lay // 2, n_lay)
-
+    load_bc.wait()
+    for i in lefts:
+        x1[i].wait_recv()
+    n_tiles = (el + 128) // 256
+
+    def project(pairs, weight, w0, t0):
+        lhs = jnp.concatenate(
+            [rows_all[pl.ds(yy * 2, 2)].reshape(2 * rows, d) for yy in pairs], axis=0
+        )
+        term = jnp.dot(lhs, weight[:, pl.ds(w0, 256)], preferred_element_type=F32)
+        for k, yy in enumerate(pairs):
+            at = pl.ds(pl.multiple_of(8 + yy * 2 * rows, 8), 2 * rows)
+            pre[at, pl.ds(t0, 256)] = term[k * 2 * rows : (k + 1) * 2 * rows]
+
+    def project_own(t):
+        if t < n_tiles:
+            project((y,), w_x, t * 256, t * 256)
+        elif t == n_tiles:
+            project((y,), w_bc, 0, el + 128)
+
+    project_own(0)
+    project_own(1)
     u3, d3, x4 = {}, {}, {}
     for i in every:
         if i in rights:
@@ -251,37 +279,25 @@
             u2[i].wait_recv()
             d2[i].wait_recv()
             x4[i] = hop(far, xl, i, at_x)
+        if i == 1:
+            project_own(2)
+    project_own(3)
 
     id_edge.wait_recv()
     idc[0:8, :] = jnp.where(seq > 0, idc[0:8, :], -1.0)
-    loads[2].wait()
     n_half = n_tp // 2
     m_half = n_half * rows
-
-    def project(weight, w0, w, target, t0, r0, i):
-        for j in range(2):
-            lhs = rows_all[n_half * j : n_half * (j + 1), :, cols[i]].reshape(
-                m_half, pieces[i][1]
-            )
-            at = (pl.ds(r0 + j * m_half, m_half), pl.ds(t0, w))
-            term = jnp.dot(lhs, weight[cols[i], pl.ds(w0, w)], preferred_element_type=F32)
-            target[at] = term if i == 0 else target[at] + term
-
     for i in every:
-        if i in rights:
-            u3[i].wait_recv()
-            d3[i].wait_recv()
-        else:
-            for copy in (x1[i], x2[i], x3[i], x4[i]):
-                copy.wait_recv()
-
-        def step(t, carry, i=i):
-            c0 = pl.multiple_of(t * 256, 256)
-            project(w_x, c0, 256, pre, c0, 8, i)
-            return carry
-
-        lax.fori_loop(0, (el + 128) // 256, step, 0)
-        project(w_bc, 0, 256, pre, el + 128, 8, i)
+        for copy in (u3[i], d3[i]) if i in rights else (x2[i], x3[i], x4[i]):
+            copy.wait_recv()
+
+    def step(t, carry):
+        c0 = pl.multiple_of(t * 256, 256)
+        project((up, far, down), w_x, c0, c0)
+        return carry
+
+    lax.fori_loop(0, n_tiles, step, 0)
+    project((up, far, down), w_bc, 0, el + 128)
 
     step_all = jax.nn.softplus(pre[8 : 8 + toks, el : el + 128] + prm[0:1, :])
     dtp[...] = step_all
@@ -320,7 +336,7 @@
             )
 
     gate_tiles = [(c0, min(256, el - c0)) for c0 in range(0, el, 256)]
-    for tile in gate_tiles[:-1]:
+    for tile in gate_tiles[:-2]:
         project_gate(*tile)
 
     edge.wait_recv()
@@ -377,11 +393,12 @@
         grams[b] = jnp.where(same & (ti >= si), gram, 0.0)
 
     state_copies = []
-    for k in range(1, n_seq):
+    for k in far_first:
         peer = lax.rem(seq + k, n_seq)
         state_copies.append(push(a_out.at[peer], a_in.at[seq], {"seq": peer}))
     a_in[seq] = a_out[seq]
-    project_gate(*gate_tiles[-1])
+    for tile in gate_tiles[-2:]:
+        project_gate(*tile)
     for b in range(n_blocks):
         r0 = b * BLOCK
         xp[r0 : r0 + BLOCK, :] = (
@@ -428,29 +445,35 @@
         keep = decay[k0 : k0 + 1, :] + decay[k0 + 1 : k0 + 2, :] + decay[k0 + 2 : k0 + 3, :]
         run = keep * run + a_in[s, :, 0:el].astype(F32)
     back_copies = []
-    for k in range(1, n_seq):
+    for k in far_first:
         peer = lax.rem(seq + k, n_seq)
         back_copies.append(push(i_out.at[peer], i_in.at[seq], {"seq": peer}))
     i_in[seq] = i_out[seq]
     for b in range(1, n_blocks):
         inside(b)
-    loads[3].wait()
-
-    for copy in back_copies:
-        copy.wait_recv()
-
-    state = i_in[...].astype(F32).reshape(128, el)
+    load_out.wait()
+
     skip = lanes_of(jnp.broadcast_to(prm[2:3, :], (8, 128)), spread)[0:1, :]
     for b in range(n_blocks):
         r0 = b * BLOCK
+        rs = slice(r0, r0 + BLOCK)
         seg = idc[8 + r0 : 8 + r0 + BLOCK, :]
         prev = idc[7 + r0 : 8 + r0, :]
-        reach = lanes_of(jnp.exp(ldb[b]) * jnp.where(seg == prev, 1.0, 0.0), spread)
+        acc[rs, :] = acc[rs, :] + skip * xc[rs, :]
+        gate[rs, :] = jax.nn.silu(gate[rs, :])
+        xc[rs, :] = lanes_of(jnp.exp(ldb[b]) * jnp.where(seg == prev, 1.0, 0.0), spread)
+
+    for copy in back_copies:
+        copy.wait_recv()
+
+    state = i_in[...].astype(F32).reshape(128, el)
+    for b in range(n_blocks):
+        r0 = b * BLOCK
         inter = jnp.dot(
             bcm[r0 : r0 + BLOCK, 128:256], state.astype(BF16), preferred_element_type=F32
         )
-        out = acc[r0 : r0 + BLOCK, :] + reach * inter + skip * xc[r0 : r0 + BLOCK, :]
-        gated = out * jax.nn.silu(gate[r0 : r0 + BLOCK, :])
+        out = acc[r0 : r0 + BLOCK, :] + xc[r0 : r0 + BLOCK, :] * inter
+        gated = out * gate[r0 : r0 + BLOCK, :]
         sq = jnp.sum(gated * gated, axis=1, keepdims=True)
         xp[r0 : r0 + BLOCK, :] = (gated * gated_gain[...]).astype(BF16)
         for q in range(2):
@@ -458,7 +481,15 @@
             sq_out[b * 2 + q] = col.T[0:8, :]
         state = keep_lanes[b] * state + st[b]
 
-    def out_cols(i):
+    def mine(xx):
+        return pl.ds(pl.multiple_of(xx * rows, rows), rows)
+
+    zero, one = pl.ds(0, rows), pl.ds(rows, rows)
+    r2u, r2d, r3u, r3d, r4u, r4d, x6 = {}, {}, {}, {}, {}, {}, {}
+    lx = {}
+    l2u, l2d, l3u, l3d = {}, {}, {}, {}
+
+    def out_cols(i, between):
         for q in range(2):
             term = jnp.dot(
                 xp[q * m_half : (q + 1) * m_half, :],
@@ -468,41 +499,47 @@
             part[q * (n_y // 2) : (q + 1) * (n_y // 2), :, cols[i]] = term.reshape(
                 n_y // 2, 2 * rows, pieces[i][1]
             )
-
-    def mine(xx):
-        return pl.ds(pl.multiple_of(xx * rows, rows), rows)
-
-    zero, one = pl.ds(0, rows), pl.ds(rows, rows)
-    r2u, r2d, r3u, r3d, r4u, r4d, x6 = {}, {}, {}, {}, {}, {}, {}
-    lx = {}
-    l2u, l2d, l3u, l3d = {}, {}, {}, {}
+            if q == 0:
+                between()
+
+    def cross(i, yy):
+        lx[i, len([k for k in lx if k[0] == i])] = push(
+            part.at[yy, mine(other), cols[i]], xl_in.at[yy, :, cols[i]], at_x
+        )
+
+    def send_r3(i):
+        r3u[i] = push(part.at[up, one, cols[i]], yr1.at[0, 1, :, cols[i]], at_up)
+        r3d[i] = push(part.at[down, zero, cols[i]], yr1.at[1, 0, :, cols[i]], at_down)
 
     def first_sends(i):
         if i in rights:
             r2u[i] = push(part.at[far, zero, cols[i]], yr2.at[0, :, cols[i]], at_up)
             r2d[i] = push(part.at[far, one, cols[i]], yr2.at[1, :, cols[i]], at_down)
+            if i == rights[0]:
+                send_r3(i)
         else:
-            lx[i] = [
-                push(part.at[yy, mine(other), cols[i]], xl_in.at[yy, :, cols[i]], at_x)
-                for yy in (far, up, down, y)
-            ]
-
-    def second_sends(i):
-        r3u[i] = push(part.at[up, one, cols[i]], yr1.at[0, 1, :, cols[i]], at_up)
-        r3d[i] = push(part.at[down, zero, cols[i]], yr1.at[1, 0, :, cols[i]], at_down)
+            cross(i, far)
+            if i == lefts[0]:
+                cross(i, up)
+            if i == lefts[-1]:
+                for yy in (up, down, y):
+                    for j in lefts:
+                        if not (yy is up and j == lefts[0]):
+                            cross(j, yy)
+
+    sq_copies = []
+
+    def send_sq():
+        for k in range(1, n_tp):
+            peer = lax.rem(tp + k, n_tp)
+            sq_copies.append(push(sq_out.at[peer // 2], sq_in.at[tp], {"tp": peer}))
 
     for i in every:
-        out_cols(i)
-        if i > 0:
-            first_sends(i - 1)
-    sq_copies = []
-    for k in range(1, n_tp):
-        peer = lax.rem(tp + k, n_tp)
-        sq_copies.append(push(sq_out.at[peer // 2], sq_in.at[tp], {"tp": peer}))
+        out_cols(i, (lambda: first_sends(i - 1)) if i else send_sq)
     sq_in[tp] = sq_out[y]
     first_sends(len(pieces) - 1)
-    for i in rights:
-        second_sends(i)
+    for i in rights[1:2]:
+        send_r3(i)
 
     def sum_of(*refs):
         tot = refs[0].astype(F32)
@@ -517,28 +554,41 @@
             qr[0, :, c] = sum_of(part[up, zero, c], yr2[0, :, c]).astype(BF16)
             r2d[i].wait_recv()
             qr[1, :, c] = sum_of(part[down, one, c], yr2[1, :, c]).astype(BF16)
+            if i in rights[2:]:
+                send_r3(i)
             r4u[i] = push(qr.at[0, :, c], yr1.at[0, 0, :, c], at_up)
             r4d[i] = push(qr.at[1, :, c], yr1.at[1, 1, :, c], at_down)
         else:
-            lx[i][0].wait_recv()
+            lx[i, 0].wait_recv()
             ql[far, :, c] = sum_of(part[far, mine(xl), c], xl_in[far, :, c]).astype(BF16)
             l2u[i] = push(ql.at[far, pl.ds(0, half), c], yl2.at[0, :, c], at_up)
             l2d[i] = push(ql.at[far, pl.ds(half, half), c], yl2.at[1, :, c], at_down)
 
-    for i in lefts:
+    def right_sum(xx, c):
+        return sum_of(part[y, mine(xx), c], yr1[0, xx, :, c], yr1[1, xx, :, c])
+
+    for i in every:
         c = cols[i]
-        lx[i][1].wait_recv()
-        q_up = sum_of(part[up, mine(xl), c], xl_in[up, :, c])
-        lx[i][2].wait_recv()
-        q_down = sum_of(part[down, mine(xl), c], xl_in[down, :, c])
-        l2u[i].wait_recv()
-        ql[up, pl.ds(0, half), c] = (q_up[0:half] + yl2[0, :, c].astype(F32)).astype(BF16)
-        ql[up, pl.ds(half, half), c] = q_up[half:].astype(BF16)
-        l2d[i].wait_recv()
-        ql[down, pl.ds(0, half), c] = q_down[0:half].astype(BF16)
-        ql[down, pl.ds(half, half), c] = (q_down[half:] + yl2[1, :, c].astype(F32)).astype(BF16)
-        l3u[i] = push(ql.at[up, :, c], yl1.at[0, :, c], at_up)
-        l3d[i] = push(ql.at[down, :, c], yl1.at[1, :, c], at_down)
+        if i in rights:
+            for copy in (r3u[i], r3d[i], r4u[i], r4d[i]):
+                copy.wait_recv()
+            qx[:, c] = right_sum(other, c).astype(BF16)
+            x6[i] = push(qx.at[:, c], xr_in.at[:, c], at_x)
+        else:
+            lx[i, 1].wait_recv()
+            q_up = sum_of(part[up, mine(xl), c], xl_in[up, :, c])
+            lx[i, 2].wait_recv()
+            q_down = sum_of(part[down, mine(xl), c], xl_in[down, :, c])
+            l2u[i].wait_recv()
+            ql[up, pl.ds(0, half), c] = (q_up[0:half] + yl2[0, :, c].astype(F32)).astype(BF16)
+            ql[up, pl.ds(half, half), c] = q_up[half:].astype(BF16)
+            l2d[i].wait_recv()
+            ql[down, pl.ds(0, half), c] = q_down[0:half].astype(BF16)
+            ql[down, pl.ds(half, half), c] = (q_down[half:] + yl2[1, :, c].astype(F32)).astype(
+                BF16
+            )
+            l3u[i] = push(ql.at[up, :, c], yl1.at[0, :, c], at_up)
+            l3d[i] = push(ql.at[down, :, c], yl1.at[1, :, c], at_down)
 
     for copy in sq_copies:
         copy.wait_recv()
@@ -548,48 +598,33 @@
     sqc[...] = jnp.broadcast_to(tot[0:1, :], (128, 128)).T
     factor = lax.rsqrt(sqc[mine(xl), :][:, 0:1] / (el * n_tp) + EPS)
 
-    def right_sum(xx, c):
-        return sum_of(part[y, mine(xx), c], yr1[0, xx, :, c], yr1[1, xx, :, c])
-
-    for i in rights:
-        c = cols[i]
-        for copy in (r3u[i], r3d[i], r4u[i], r4d[i]):
-            copy.wait_recv()
-        qx[:, c] = right_sum(other, c).astype(BF16)
-        x6[i] = push(qx.at[:, c], xr_in.at[:, c], at_x)
-
     def finish(i, total):
         c = cols[i]
         result[:, c] = (hid[:, c].astype(F32) + factor * total).astype(BF16)
 
-    done = []
-
     def hand(i):
-        done.append(i)
-
         @pl.when(pipe == 0)
         def _():
             handoff[i].start()
 
-    for i in lefts:
+    for i in every:
         c = cols[i]
-        lx[i][3].wait_recv()
-        l3u[i].wait_recv()
-        l3d[i].wait_recv()
-        finish(i, sum_of(part[y, mine(xl), c], xl_in[y, :, c], yl1[0, :, c], yl1[1, :, c]))
-    waiting = list(lefts)
-    for i in rights:
-        c = cols[i]
-        own = right_sum(xl, c)
-        x6[i].wait_recv()
-        for j in waiting:
-            hand(j)
-        finish(i, own + xr_in[:, c].astype(F32))
-        waiting = [i]
-    for j in waiting:
-        hand(j)
-
-    for copy in sent:
+        if i in rights:
+            own = right_sum(xl, c)
+            x6[i].wait_recv()
+            finish(i, own + xr_in[:, c].astype(F32))
+        else:
+            own = sum_of(part[y, mine(xl), c])
+            for copy in (lx[i, 3], l3u[i], l3d[i]):
+                copy.wait_recv()
+            finish(i, own + sum_of(xl_in[y, :, c], yl1[0, :, c], yl1[1, :, c]))
+        if i:
+            hand(i - 1)
+
+    for copy in sent[:8]:
+        copy.wait_send()
+    hand(len(pieces) - 1)
+    for copy in sent[8:]:
         copy.wait_send()
 
     @pl.when(pipe == 0)
@@ -668,7 +703,7 @@
         pltpu.VMEM((128, 128), F32),
         pltpu.SemaphoreType.DMA((n_msg,)),
         pltpu.SemaphoreType.DMA((n_msg,)),
-        pltpu.SemaphoreType.DMA((5,)),
+        pltpu.SemaphoreType.DMA((6,)),
     ]
     out = pl.pallas_call(
         functools.partial(layer_kernel, geo),

time: 122 us -> 114 us (0.934)
  Pallas kernels: 120 us -> 112 us
    pallas_call x1, Pallas kernels: 120 us -> 112 us  [local(): pl.pallas_call(functools.partial(layer_kernel, geo), out_shape=jax.ShapeD...]
where the time goes in v3:
time: 114 us; the launch traced here: 113 us
  Pallas kernels  112 us (98%)
  local copies, waits for them, and re-layouts  1.72 us (2%)
    pallas_call x1, Pallas kernels, local(): pl.pallas_call(functools.partial(layer_kernel, geo), out_shape=jax.ShapeD...  112 us

profile of v3, /device:TPU:1, one launch (start us, length us, event | category | flops | bytes accessed | tf_op | source)
XLA Modules:
  0.0 113.5 jit_solution(7888584936527293498)
XLA Ops:
  0.0 111.7 %mixer_section.1 = bf16[64,2560]{1,0:T(8,128)(2,1)} custom-call(bf16[64,2560]{1,0:T(8,128)(2,1)} %bitcast.14, s32[1,512]{1,0:T(1,128)} %ids_ref.1, f32[1,2560]{1,0:T(1,128)} %norm_gain.1, bf16[2560,2,640]{2,1,0:T(2,128)(2,1)} %bitcast.10, bf16[2560,256]{1,0:T(8,128)(2,1)} %bitcast.13, bf16[10,2560]{1,0:T(8,128)(2,1)} %bitcast.15, f32[4,640]{1,0:T(4,128)} %bitcast.16, ...), custom_call_target="tpu_custom_call" | custom-call | tf_op jit(solution)/shard_map/mixer_section/pallas_call | solution.py:708
  111.7 1.7 %copy.17 = bf16[1,1,64,2560]{3,2,1,0:T(8,128)(2,1)} copy(bf16[1,1,64,2560]{3,2,1,0:T(8,128)(2,1)} %bitcast.12) | data formatting | bytes 655360

commit v4 on v3

--- a/solution.py
+++ b/solution.py
@@ -46,7 +46,8 @@
     w_bc,
     w_dt,
     w_out,
-    hid,
+    rows_pre,
+    rows_in,
     rows_all,
     pre,
     gate,
@@ -85,7 +86,7 @@
     pipe, seq, tp = lax.axis_index("pipe"), lax.axis_index("seq"), lax.axis_index("tp")
     y, xl = tp // 2, tp % 2
     other = 1 - xl
-    rows = hid.shape[0]
+    rows = rows_in.shape[1]
     toks = n_tp * rows
     half = rows // 2
     n_blocks = toks // BLOCK
@@ -134,9 +135,9 @@
             ]
         )
     ]
-    first_load = pltpu.make_async_copy(hidden_hbm, hid, load_sem.at[5])
-
-    @pl.when(pipe == 0)
+    first_load = pltpu.make_async_copy(hidden_hbm, rows_pre.at[tp], load_sem.at[5])
+
+    @pl.when(pipe == 1)
     def _():
         first_load.start()
 
@@ -195,109 +196,179 @@
     n_lay = d // 64
     load_dt.wait()
     lay_out_dt()
-    load_top.wait()
-    lay_out(0, n_lay // 2)
+
+    @pl.when(pipe == 0)
+    def _():
+        load_top.wait()
+        lay_out(0, n_lay // 2)
+        load_bottom.wait()
+        lay_out(n_lay // 2, n_lay)
+        load_bc.wait()
 
     pl.semaphore_wait(barrier, n_tp + n_seq - 1)
     id_edge = push(idc.at[pl.ds(toks, 8)], idc.at[pl.ds(0, 8)], nxt)
-    handoff = [remote(result.at[:, c], hid.at[:, c], {"pipe": 1 - pipe}) for c in cols]
+    mate = {"pipe": 1 - pipe}
+    handoff = [remote(result.at[:, c], rows_in.at[tp, :, c], mate) for c in cols]
+
+    def norm_rows(yy):
+        for xx in range(2):
+            t = yy * 2 + xx
+            h = rows_in[t].astype(F32)
+            scale = lax.rsqrt(jnp.mean(h * h, axis=1, keepdims=True) + EPS)
+            rows_all[t] = (h * scale * norm_gain[...]).astype(BF16)
+
+    tiles = [(w_x, c0, c0) for c0 in range(0, el + 128, 256)] + [(w_bc, 0, el + 128)]
+    tile_groups = [tiles[k : k + 2] for k in range(0, len(tiles), 2)]
+
+    def project(pairs, group):
+        lhs = jnp.concatenate(
+            [rows_all[pl.ds(yy * 2, 2)].reshape(2 * rows, d) for yy in pairs], axis=0
+        )
+        for weight, w0, t0 in group:
+            term = jnp.dot(lhs, weight[:, w0 : w0 + 256], preferred_element_type=F32)
+            for k, yy in enumerate(pairs):
+                at = pl.ds(pl.multiple_of(8 + yy * 2 * rows, 8), 2 * rows)
+                pre[at, t0 : t0 + 256] = term[k * 2 * rows : (k + 1) * 2 * rows]
+
+    def gather(buf, ready, early, middle, late, last):
+        mine_sent = []
+
+        def hop(yy, xx, i, where, r0=0, n=rows):
+            s = buf.at[yy * 2 + xx, pl.ds(r0, n), cols[i]]
+            copy = remote(s, s, where)
+            copy.start()
+            mine_sent.append(copy)
+            return copy
+
+        u1, d1, x1 = {}, {}, {}
+        for i in every:
+            ready(i)
+            u1[i], d1[i] = hop(y, xl, i, at_up), hop(y, xl, i, at_down)
+            x1[i] = hop(y, xl, i, at_x)
+        u2, d2, x2, x3 = {}, {}, {}, {}
+        for i in every:
+            if i in rights:
+                x1[i].wait_recv()
+                u2[i], d2[i] = hop(y, other, i, at_up), hop(y, other, i, at_down)
+            else:
+                u1[i].wait_recv()
+                u2[i] = hop(down, xl, i, at_up, 0, half)
+                x2[i] = hop(down, xl, i, at_x)
+                d1[i].wait_recv()
+                d2[i] = hop(up, xl, i, at_down, half, half)
+                x3[i] = hop(up, xl, i, at_x)
+        for i in every:
+            if i in rights:
+                u1[i].wait_recv()
+                d1[i].wait_recv()
+            else:
+                x1[i].wait_recv()
+        early()
+        u3, d3, x4 = {}, {}, {}
+        for i in every:
+            if i in rights:
+                u2[i].wait_recv()
+                u3[i] = hop(down, 0, i, at_up)
+                d2[i].wait_recv()
+                d3[i] = hop(up, 1, i, at_down)
+            else:
+                u2[i].wait_recv()
+                d2[i].wait_recv()
+                x4[i] = hop(far, xl, i, at_x)
+            if i == 1:
+                middle()
+        for i in lefts:
+            x2[i].wait_recv()
+            x3[i].wait_recv()
+        late()
+        for i in every:
+            for copy in (u3[i], d3[i]) if i in rights else (x4[i],):
+                copy.wait_recv()
+            last(i)
+        return mine_sent
+
+    def pair_of(yy):
+        return pl.ds(yy * 2, 2)
+
+    def across(at):
+        return remote(rows_pre.at[at], rows_in.at[at], mate)
+
+    own_pair = across(pair_of(y))
+    near = [across(yy * 2 + xl) for yy in (down, up)]
+    beside = [across(yy * 2 + other) for yy in (down, up)]
+    rest = [
+        remote(rows_pre.at[pair_of(far), :, c], rows_in.at[pair_of(far), :, c], mate)
+        for c in cols
+    ]
+
+    @pl.when(pipe == 1)
+    def _():
+        first_load.wait()
+
+        def early():
+            for copy in [own_pair] + near:
+                copy.start()
+
+        def late():
+            for copy in beside:
+                copy.start()
+
+        first = gather(
+            rows_pre, lambda i: None, early, lambda: None, late, lambda i: rest[i].start()
+        )
+        load_top.wait()
+        load_bottom.wait()
+        lay_out(0, n_lay)
+        load_bc.wait()
+        for copy in first + [own_pair] + near + beside + rest:
+            copy.wait_send()
+
+    @pl.when(pipe == 1)
+    def _():
+        def early():
+            norm_rows(y)
+            project((y,), tile_groups[0])
+
+        def middle():
+            for group in tile_groups[1:]:
+                project((y,), group)
+
+        def late():
+            norm_rows(down)
+            norm_rows(up)
+
+        second = gather(
+            rows_in,
+            lambda i: handoff[i].wait_recv(),
+            early,
+            middle,
+            late,
+            lambda i: None,
+        )
+        norm_rows(far)
+        for group in tile_groups:
+            project((up, far, down), group)
+        for copy in second:
+            copy.wait_send()
 
     @pl.when(pipe == 0)
     def _():
-        first_load.wait()
-
-    load_bottom.wait()
-
-    @pl.when(pipe == 1)
-    def _():
-        lay_out(n_lay // 2, n_lay)
-        for copy in handoff:
-            copy.wait_recv()
-
-    h = hid[...].astype(F32)
-    scale = lax.rsqrt(jnp.mean(h * h, axis=1, keepdims=True) + EPS)
-    rows_all[tp] = (h * scale * norm_gain[...]).astype(BF16)
-
-    def hop(yy, xx, i, where, r0=0, n=rows):
-        s = rows_all.at[yy * 2 + xx, pl.ds(r0, n), cols[i]]
-        return push(s, s, where)
-
-    u1, d1, x1 = {}, {}, {}
-    for i in every:
-        u1[i], d1[i] = hop(y, xl, i, at_up), hop(y, xl, i, at_down)
-        x1[i] = hop(y, xl, i, at_x)
-
-    @pl.when(pipe == 0)
-    def _():
-        lay_out(n_lay // 2, n_lay)
-
-    u2, d2, x2, x3 = {}, {}, {}, {}
-    for i in every:
-        if i in rights:
-            x1[i].wait_recv()
-            u2[i], d2[i] = hop(y, other, i, at_up), hop(y, other, i, at_down)
-        else:
-            u1[i].wait_recv()
-            u2[i] = hop(down, xl, i, at_up, 0, half)
-            x2[i] = hop(down, xl, i, at_x)
-            d1[i].wait_recv()
-            d2[i] = hop(up, xl, i, at_down, half, half)
-            x3[i] = hop(up, xl, i, at_x)
-
-    load_bc.wait()
-    for i in lefts:
-        x1[i].wait_recv()
-    n_tiles = (el + 128) // 256
-
-    def project(pairs, weight, w0, t0):
-        lhs = jnp.concatenate(
-            [rows_all[pl.ds(yy * 2, 2)].reshape(2 * rows, d) for yy in pairs], axis=0
-        )
-        term = jnp.dot(lhs, weight[:, pl.ds(w0, 256)], preferred_element_type=F32)
-        for k, yy in enumerate(pairs):
-            at = pl.ds(pl.multiple_of(8 + yy * 2 * rows, 8), 2 * rows)
-            pre[at, pl.ds(t0, 256)] = term[k * 2 * rows : (k + 1) * 2 * rows]
-
-    def project_own(t):
-        if t < n_tiles:
-            project((y,), w_x, t * 256, t * 256)
-        elif t == n_tiles:
-            project((y,), w_bc, 0, el + 128)
-
-    project_own(0)
-    project_own(1)
-    u3, d3, x4 = {}, {}, {}
-    for i in every:
-        if i in rights:
-            u1[i].wait_recv()
-            u2[i].wait_recv()
-            u3[i] = hop(down, 0, i, at_up)
-            d1[i].wait_recv()
-            d2[i].wait_recv()
-            d3[i] = hop(up, 1, i, at_down)
-        else:
-            u2[i].wait_recv()
-            d2[i].wait_recv()
-            x4[i] = hop(far, xl, i, at_x)
-        if i == 1:
-            project_own(2)
-    project_own(3)
+        for copies, yy in (
+            ([own_pair], y),
+            ([near[0], beside[0]], down),
+            ([near[1], beside[1]], up),
+            (rest, far),
+        ):
+            for copy in copies:
+                copy.wait_recv()
+            norm_rows(yy)
+            for group in tile_groups:
+                project((yy,), group)
 
     id_edge.wait_recv()
     idc[0:8, :] = jnp.where(seq > 0, idc[0:8, :], -1.0)
     n_half = n_tp // 2
     m_half = n_half * rows
-    for i in every:
-        for copy in (u3[i], d3[i]) if i in rights else (x2[i], x3[i], x4[i]):
-            copy.wait_recv()
-
-    def step(t, carry):
-        c0 = pl.multiple_of(t * 256, 256)
-        project((up, far, down), w_x, c0, c0)
-        return carry
-
-    lax.fori_loop(0, n_tiles, step, 0)
-    project((up, far, down), w_bc, 0, el + 128)
 
     step_all = jax.nn.softplus(pre[8 : 8 + toks, el : el + 128] + prm[0:1, :])
     dtp[...] = step_all
@@ -600,7 +671,7 @@
 
     def finish(i, total):
         c = cols[i]
-        result[:, c] = (hid[:, c].astype(F32) + factor * total).astype(BF16)
+        result[:, c] = (rows_in[tp, :, c].astype(F32) + factor * total).astype(BF16)
 
     def hand(i):
         @pl.when(pipe == 0)
@@ -659,7 +730,7 @@
     n_right = sum(1 for p in pieces if p[2])
     n_left = len(pieces) - n_right
     n_msg = (
-        2 + len(pieces) + 2 * (n_seq - 1) + (n_tp - 1) + 14 * n_right + 16 * n_left
+        7 + 2 * len(pieces) + 2 * (n_seq - 1) + (n_tp - 1) + 21 * n_right + 24 * n_left
     )
     vmem = pl.BlockSpec(memory_space=pltpu.VMEM)
     anyw = pl.BlockSpec(memory_space=pl.ANY)
@@ -670,7 +741,8 @@
         pltpu.VMEM((d, 256), BF16),
         pltpu.VMEM((nh, d), BF16),
         pltpu.VMEM((el, d), BF16),
-        pltpu.VMEM((rows, d), BF16),
+        pltpu.VMEM((n_tp, rows, d), BF16),
+        pltpu.VMEM((n_tp, rows, d), BF16),
         pltpu.VMEM((n_tp, rows, d), BF16),
         pltpu.VMEM((toks + 8, el + 384), F32),
         pltpu.VMEM((toks, el), F32),

time: 114 us -> 107 us (0.939)
  Pallas kernels: 112 us -> 105 us
    pallas_call x1, Pallas kernels: 112 us -> 105 us  [local(): pl.pallas_call(functools.partial(layer_kernel, geo), out_shape=jax.ShapeD...]
where the time goes in v4:
time: 107 us
  Pallas kernels  105 us (98%)
  local copies, waits for them, and re-layouts  1.72 us (2%)
    pallas_call x1, Pallas kernels, local(): pl.pallas_call(functools.partial(layer_kernel, geo), out_shape=jax.ShapeD...  105 us

profile of v4, /device:TPU:1, one launch (start us, length us, event | category | flops | bytes accessed | tf_op | source)
XLA Modules:
  0.0 106.6 jit_solution(4250697951039661231)
XLA Ops:
  0.0 104.9 %mixer_section.1 = bf16[64,2560]{1,0:T(8,128)(2,1)} custom-call(bf16[64,2560]{1,0:T(8,128)(2,1)} %bitcast.14, s32[1,512]{1,0:T(1,128)} %ids_ref.1, f32[1,2560]{1,0:T(1,128)} %norm_gain.1, bf16[2560,2,640]{2,1,0:T(2,128)(2,1)} %bitcast.10, bf16[2560,256]{1,0:T(8,128)(2,1)} %bitcast.13, bf16[10,2560]{1,0:T(8,128)(2,1)} %bitcast.15, f32[4,640]{1,0:T(4,128)} %bitcast.16, ...), custom_call_target="tpu_custom_call" | custom-call | tf_op jit(solution)/shard_map/mixer_section/pallas_call | solution.py:780
  104.9 1.7 %copy.17 = bf16[1,1,64,2560]{3,2,1,0:T(8,128)(2,1)} copy(bf16[1,1,64,2560]{3,2,1,0:T(8,128)(2,1)} %bitcast.12) | data formatting | bytes 655360

commit v5 on v4

--- a/solution.py
+++ b/solution.py
@@ -98,9 +98,9 @@
     at_x = {"tp": y * 2 + other}
     nxt = {"seq": lax.rem(seq + 1, n_seq)}
     every = range(len(pieces))
-    rights = [i for i in every if pieces[i][2]]
-    lefts = [i for i in every if not pieces[i][2]]
-    cols = [pl.ds(c0, w) for c0, w, _ in pieces]
+    rights = [i for i in every if pieces[i][3]]
+    lefts = [i for i in every if not pieces[i][3]]
+    cols = [pl.ds(c0, w) for c0, w, _, _ in pieces]
     counter = [0]
     sent = []
 
@@ -144,7 +144,7 @@
     for copy in loads:
         copy.start()
 
-    far_first = sorted(range(1, n_seq), key=lambda k: abs(2 * k - n_seq))
+    far_first = sorted(range(1, n_seq), key=lambda k: (k % 2 == 0, abs(2 * k - n_seq)))
     barrier = pltpu.get_barrier_semaphore()
     for k in far_first:
         pl.semaphore_signal(
@@ -194,11 +194,11 @@
             ).astype(BF16)
 
     n_lay = d // 64
-    load_dt.wait()
-    lay_out_dt()
 
     @pl.when(pipe == 0)
     def _():
+        load_dt.wait()
+        lay_out_dt()
         load_top.wait()
         lay_out(0, n_lay // 2)
         load_bottom.wait()
@@ -210,9 +210,13 @@
     mate = {"pipe": 1 - pipe}
     handoff = [remote(result.at[:, c], rows_in.at[tp, :, c], mate) for c in cols]
 
-    def norm_rows(yy):
-        for xx in range(2):
-            t = yy * 2 + xx
+    own_rows = (y * 2, y * 2 + 1)
+    near_rows = (down * 2 + xl, up * 2 + xl)
+    beside_rows = (down * 2 + other, up * 2 + other)
+    far_rows = (far * 2, far * 2 + 1)
+
+    def norm_rows(slots):
+        for t in slots:
             h = rows_in[t].astype(F32)
             scale = lax.rsqrt(jnp.mean(h * h, axis=1, keepdims=True) + EPS)
             rows_all[t] = (h * scale * norm_gain[...]).astype(BF16)
@@ -220,17 +224,20 @@
     tiles = [(w_x, c0, c0) for c0 in range(0, el + 128, 256)] + [(w_bc, 0, el + 128)]
     tile_groups = [tiles[k : k + 2] for k in range(0, len(tiles), 2)]
 
-    def project(pairs, group):
-        lhs = jnp.concatenate(
-            [rows_all[pl.ds(yy * 2, 2)].reshape(2 * rows, d) for yy in pairs], axis=0
-        )
+    def project(slots, group):
+        lhs = jnp.concatenate([rows_all[t] for t in slots], axis=0)
         for weight, w0, t0 in group:
             term = jnp.dot(lhs, weight[:, w0 : w0 + 256], preferred_element_type=F32)
-            for k, yy in enumerate(pairs):
-                at = pl.ds(pl.multiple_of(8 + yy * 2 * rows, 8), 2 * rows)
-                pre[at, t0 : t0 + 256] = term[k * 2 * rows : (k + 1) * 2 * rows]
-
-    def gather(buf, ready, early, middle, late, last):
+            for k, t in enumerate(slots):
+                at = pl.ds(pl.multiple_of(8 + t * rows, 8), rows)
+                pre[at, t0 : t0 + 256] = term[k * rows : (k + 1) * rows]
+
+    def take(slots):
+        norm_rows(slots)
+        for group in tile_groups:
+            project(slots, group)
+
+    def gather(buf, ready, early, late, last):
         mine_sent = []
 
         def hop(yy, xx, i, where, r0=0, n=rows):
@@ -247,7 +254,7 @@
             x1[i] = hop(y, xl, i, at_x)
         u2, d2, x2, x3 = {}, {}, {}, {}
         for i in every:
-            if i in rights:
+            if pieces[i][2]:
                 x1[i].wait_recv()
                 u2[i], d2[i] = hop(y, other, i, at_up), hop(y, other, i, at_down)
             else:
@@ -258,7 +265,7 @@
                 d2[i] = hop(up, xl, i, at_down, half, half)
                 x3[i] = hop(up, xl, i, at_x)
         for i in every:
-            if i in rights:
+            if pieces[i][2]:
                 u1[i].wait_recv()
                 d1[i].wait_recv()
             else:
@@ -266,7 +273,7 @@
         early()
         u3, d3, x4 = {}, {}, {}
         for i in every:
-            if i in rights:
+            if pieces[i][2]:
                 u2[i].wait_recv()
                 u3[i] = hop(down, 0, i, at_up)
                 d2[i].wait_recv()
@@ -275,14 +282,12 @@
                 u2[i].wait_recv()
                 d2[i].wait_recv()
                 x4[i] = hop(far, xl, i, at_x)
-            if i == 1:
-                middle()
-        for i in lefts:
+        for i in x2:
             x2[i].wait_recv()
             x3[i].wait_recv()
         late()
         for i in every:
-            for copy in (u3[i], d3[i]) if i in rights else (x4[i],):
+            for copy in (u3[i], d3[i]) if pieces[i][2] else (x4[i],):
                 copy.wait_recv()
             last(i)
         return mine_sent
@@ -314,8 +319,10 @@
                 copy.start()
 
         first = gather(
-            rows_pre, lambda i: None, early, lambda: None, late, lambda i: rest[i].start()
-        )
+            rows_pre, lambda i: None, early, late, lambda i: rest[i].start()
+        )
+        load_dt.wait()
+        lay_out_dt()
         load_top.wait()
         load_bottom.wait()
         lay_out(0, n_lay)
@@ -326,44 +333,34 @@
     @pl.when(pipe == 1)
     def _():
         def early():
-            norm_rows(y)
-            project((y,), tile_groups[0])
-
-        def middle():
-            for group in tile_groups[1:]:
-                project((y,), group)
+            take(own_rows)
 
         def late():
-            norm_rows(down)
-            norm_rows(up)
+            take(near_rows)
+            take(beside_rows)
 
         second = gather(
             rows_in,
             lambda i: handoff[i].wait_recv(),
             early,
-            middle,
             late,
             lambda i: None,
         )
-        norm_rows(far)
-        for group in tile_groups:
-            project((up, far, down), group)
+        take(far_rows)
         for copy in second:
             copy.wait_send()
 
     @pl.when(pipe == 0)
     def _():
-        for copies, yy in (
-            ([own_pair], y),
-            ([near[0], beside[0]], down),
-            ([near[1], beside[1]], up),
-            (rest, far),
+        for copies, slots in (
+            ([own_pair], own_rows),
+            (near, near_rows),
+            (beside, beside_rows),
+            (rest, far_rows),
         ):
             for copy in copies:
                 copy.wait_recv()
-            norm_rows(yy)
-            for group in tile_groups:
-                project((yy,), group)
+            take(slots)
 
     id_edge.wait_recv()
     idc[0:8, :] = jnp.where(seq > 0, idc[0:8, :], -1.0)
@@ -374,13 +371,15 @@
     dtp[...] = step_all
     edge = push(pre.at[pl.ds(toks, 8)], pre.at[pl.ds(0, 8)], nxt)
     rate = step_all * prm[1:2, :]
-    tri = jnp.where(ti >= si, 1.0, 0.0)
+    tri = jnp.where(ti >= si, 1.0, 0.0).astype(BF16)
+    r_hi = rate.astype(BF16)
+    r_rest = rate - r_hi.astype(F32)
+    r_mid = r_rest.astype(BF16)
+    r_lo = (r_rest - r_mid.astype(F32)).astype(BF16)
     for b in range(n_blocks):
-        ldb[b] = jnp.dot(
-            tri,
-            rate[b * BLOCK : (b + 1) * BLOCK],
-            precision=lax.Precision.HIGHEST,
-            preferred_element_type=F32,
+        ldb[b] = sum(
+            jnp.dot(tri, r[b * BLOCK : (b + 1) * BLOCK], preferred_element_type=F32)
+            for r in (r_lo, r_mid, r_hi)
         )
 
     def convolve(r):
@@ -390,9 +389,12 @@
         run_bc = jnp.broadcast_to(bias_bc[...], (64, 256))
         for k in range(4):
             at = r0 + 5 + k
-            keep = jnp.where(idc[at : at + 64, :][:, 0:1] == own, 1.0, 0.0)
-            run_x = run_x + keep * conv_x[k : k + 1, :] * pre[at : at + 64, 0:el]
-            run_bc = run_bc + keep * conv_bc[k : k + 1, :] * pre[at : at + 64, el + 128 :]
+            tap_x, tap_bc = conv_x[k : k + 1, :], conv_bc[k : k + 1, :]
+            if k < 3:
+                keep = jnp.where(idc[at : at + 64, :][:, 0:1] == own, 1.0, 0.0)
+                tap_x, tap_bc = keep * tap_x, keep * tap_bc
+            run_x = run_x + tap_x * pre[at : at + 64, 0:el]
+            run_bc = run_bc + tap_bc * pre[at : at + 64, el + 128 :]
         xc[r0 : r0 + 64, :] = jax.nn.silu(run_x)
         bcm[r0 : r0 + 64, :] = jax.nn.silu(run_bc).astype(BF16)
 
@@ -410,11 +412,9 @@
     for tile in gate_tiles[:-2]:
         project_gate(*tile)
 
-    edge.wait_recv()
-    convolve(0)
-
-    keeps = []
-    for b in range(n_blocks):
+    keeps = [None] * n_blocks
+
+    def states(b):
         r0 = b * BLOCK
         ld = ldb[b]
         ld_end = ld[BLOCK - 1 : BLOCK, :]
@@ -432,7 +432,13 @@
             preferred_element_type=F32,
         )
         keep = jnp.exp(ld_end) * jnp.where(seg_end == prev, 1.0, 0.0)
-        keeps.append(jnp.broadcast_to(keep, (8, 128)))
+        keeps[b] = jnp.broadcast_to(keep, (8, 128))
+
+    for b in range(1, n_blocks):
+        states(b)
+    edge.wait_recv()
+    convolve(0)
+    states(0)
     keep_lanes = [lanes_of(k, spread)[0:1, :] for k in keeps]
     total = st[0]
     keep_shard = keeps[0]
@@ -727,11 +733,9 @@
     toks = rows * n_tp
     ng = 128 // n_seq
     n_blocks = toks // BLOCK
-    n_right = sum(1 for p in pieces if p[2])
-    n_left = len(pieces) - n_right
-    n_msg = (
-        7 + 2 * len(pieces) + 2 * (n_seq - 1) + (n_tp - 1) + 21 * n_right + 24 * n_left
-    )
+    in_right = sum(1 for p in pieces if p[2])
+    out_right = sum(1 for p in pieces if p[3])
+    n_msg = 7 + 26 * len(pieces) + 2 * (n_seq - 1) + (n_tp - 1) - 2 * in_right - out_right
     vmem = pl.BlockSpec(memory_space=pltpu.VMEM)
     anyw = pl.BlockSpec(memory_space=pl.ANY)
     scratch = [
@@ -810,7 +814,9 @@
 def build(mesh, d, e, h):
     n_seq, n_tp = mesh.shape["seq"], mesh.shape["tp"]
     wide = 512 if d % 512 == 0 else 128
-    pieces = tuple((c, wide, (c // wide) % 2 == 0) for c in range(0, d, wide))
+    pieces = tuple(
+        (c, wide, (c // wide) % 2 == 0, (c // wide) % 3 != 1) for c in range(0, d, wide)
+    )
     geo = (n_seq, n_tp, n_tp // 2, d, e // n_tp, h // n_tp, pieces)
     in_specs = (
         P(None, ("seq", "tp"), None),

time: 107 us -> 105 us (0.981)
  Pallas kernels: 105 us -> 103 us
    pallas_call x1, Pallas kernels: 105 us -> 103 us  [local(): pl.pallas_call(functools.partial(layer_kernel, geo), out_shape=jax.ShapeD...]
where the time goes in v5:
time: 105 us; the launch traced here: 104 us
  Pallas kernels  103 us (98%)
  local copies, waits for them, and re-layouts  1.72 us (2%)
    pallas_call x1, Pallas kernels, local(): pl.pallas_call(functools.partial(layer_kernel, geo), out_shape=jax.ShapeD...  103 us

profile of v5, /device:TPU:1, one launch (start us, length us, event | category | flops | bytes accessed | tf_op | source)
XLA Modules:
  0.0 104.4 jit_solution(6779745368951059469)
XLA Ops:
  0.0 102.7 %mixer_section.1 = bf16[64,2560]{1,0:T(8,128)(2,1)} custom-call(bf16[64,2560]{1,0:T(8,128)(2,1)} %bitcast.14, s32[1,512]{1,0:T(1,128)} %ids_ref.1, f32[1,2560]{1,0:T(1,128)} %norm_gain.1, bf16[2560,2,640]{2,1,0:T(2,128)(2,1)} %bitcast.10, bf16[2560,256]{1,0:T(8,128)(2,1)} %bitcast.13, bf16[10,2560]{1,0:T(8,128)(2,1)} %bitcast.15, f32[4,640]{1,0:T(4,128)} %bitcast.16, ...), custom_call_target="tpu_custom_call" | custom-call | tf_op jit(solution)/shard_map/mixer_section/pallas_call | solution.py:784
  102.7 1.7 %copy.17 = bf16[1,1,64,2560]{3,2,1,0:T(8,128)(2,1)} copy(bf16[1,1,64,2560]{3,2,1,0:T(8,128)(2,1)} %bitcast.12) | data formatting | bytes 655360

commit v6 on v5

--- a/solution.py
+++ b/solution.py
@@ -237,7 +237,7 @@
         for group in tile_groups:
             project(slots, group)
 
-    def gather(buf, ready, early, late, last):
+    def gather(buf, eager, ready, early, between, late, last):
         mine_sent = []
 
         def hop(yy, xx, i, where, r0=0, n=rows):
@@ -247,13 +247,14 @@
             mine_sent.append(copy)
             return copy
 
-        u1, d1, x1 = {}, {}, {}
-        for i in every:
+        u1, d1, x1, u2, d2, x2, x3 = {}, {}, {}, {}, {}, {}, {}
+
+        def first(i):
             ready(i)
             u1[i], d1[i] = hop(y, xl, i, at_up), hop(y, xl, i, at_down)
             x1[i] = hop(y, xl, i, at_x)
-        u2, d2, x2, x3 = {}, {}, {}, {}
-        for i in every:
+
+        def second(i):
             if pieces[i][2]:
                 x1[i].wait_recv()
                 u2[i], d2[i] = hop(y, other, i, at_up), hop(y, other, i, at_down)
@@ -264,6 +265,14 @@
                 d1[i].wait_recv()
                 d2[i] = hop(up, xl, i, at_down, half, half)
                 x3[i] = hop(up, xl, i, at_x)
+
+        for i in every:
+            first(i)
+            if i == 2 and eager:
+                second(0)
+        for i in every:
+            if 0 not in u2 or i:
+                second(i)
         for i in every:
             if pieces[i][2]:
                 u1[i].wait_recv()
@@ -282,6 +291,7 @@
                 u2[i].wait_recv()
                 d2[i].wait_recv()
                 x4[i] = hop(far, xl, i, at_x)
+            between(i)
         for i in x2:
             x2[i].wait_recv()
             x3[i].wait_recv()
@@ -319,7 +329,13 @@
                 copy.start()
 
         first = gather(
-            rows_pre, lambda i: None, early, late, lambda i: rest[i].start()
+            rows_pre,
+            False,
+            lambda i: None,
+            early,
+            lambda i: None,
+            late,
+            lambda i: rest[i].start(),
         )
         load_dt.wait()
         lay_out_dt()
@@ -332,18 +348,28 @@
 
     @pl.when(pipe == 1)
     def _():
-        def early():
-            take(own_rows)
-
-        def late():
-            take(near_rows)
-            take(beside_rows)
+        chunks = {
+            0: (lambda: norm_rows(own_rows), lambda: project(own_rows, tile_groups[0])),
+            min(2, len(pieces) - 1): (
+                lambda: [project(own_rows, g) for g in tile_groups[1:]],
+                lambda: norm_rows(near_rows),
+            ),
+        }
+
+        def between(i):
+            for chunk in chunks.get(i, ()):
+                chunk()
+            if i == len(pieces) - 1:
+                for group in tile_groups:
+                    project(near_rows, group)
 
         second = gather(
             rows_in,
+            True,
             lambda i: handoff[i].wait_recv(),
-            early,
-            late,
+            lambda: None,
+            between,
+            lambda: take(beside_rows),
             lambda i: None,
         )
         take(far_rows)
@@ -680,6 +706,9 @@
         result[:, c] = (rows_in[tp, :, c].astype(F32) + factor * total).astype(BF16)
 
     def hand(i):
+        if i < 0:
+            return
+
         @pl.when(pipe == 0)
         def _():
             handoff[i].start()
@@ -688,15 +717,15 @@
         c = cols[i]
         if i in rights:
             own = right_sum(xl, c)
+            hand(i - 1)
             x6[i].wait_recv()
             finish(i, own + xr_in[:, c].astype(F32))
         else:
             own = sum_of(part[y, mine(xl), c])
+            hand(i - 1)
             for copy in (lx[i, 3], l3u[i], l3d[i]):
                 copy.wait_recv()
             finish(i, own + sum_of(xl_in[y, :, c], yl1[0, :, c], yl1[1, :, c]))
-        if i:
-            hand(i - 1)
 
     for copy in sent[:8]:
         copy.wait_send()
@@ -808,6 +837,20 @@
         gated_gain,
         out_w[0],
     )
+
+    def write(src, dst, sem):
+        copy = pltpu.make_async_copy(src, dst, sem)
+        copy.start()
+        copy.wait()
+
+    out = pl.pallas_call(
+        write,
+        out_shape=jax.ShapeDtypeStruct((rows, d), BF16),
+        in_specs=[vmem],
+        out_specs=anyw,
+        scratch_shapes=[pltpu.SemaphoreType.DMA(())],
+        name="write_rows",
+    )(out)
     return out[None, None]
 
 

time: 105 us -> 104 us (level)
  local copies, waits for them, and re-layouts: 1.72 us -> 0 us
    unnamed x1 -> x0, local copies, waits for them, and re-layouts: 1.72 us -> none
    pallas_call x0 -> x1, Pallas kernels: none -> 1.7 us  [local(): pl.pallas_call(write, out_shape=jax.ShapeDtypeStruct((rows, d), BF16), in...]
where the time goes in v6:
time: 104 us
  Pallas kernels  103 us (99%)
    pallas_call x1, Pallas kernels, local(): pl.pallas_call(functools.partial(layer_kernel, geo), out_shape=jax.ShapeD...  102 us

profile of v6, /device:TPU:1, one launch (start us, length us, event | category | flops | bytes accessed | tf_op | source)
XLA Modules:
  0.0 103.5 jit_solution(15431061848571398501)
XLA Ops:
  0.0 101.7 %mixer_section.1.src = bf16[64,2560]{1,0:T(8,128)(2,1)} custom-call(bf16[64,2560]{1,0:T(8,128)(2,1)} %bitcast.13, s32[1,512]{1,0:T(1,128)} %ids_ref.1, f32[1,2560]{1,0:T(1,128)} %norm_gain.1, bf16[2560,2,640]{2,1,0:T(2,128)(2,1)} %bitcast.10, bf16[2560,256]{1,0:T(8,128)(2,1)} %bitcast.12, bf16[10,2560]{1,0:T(8,128)(2,1)} %bitcast.14, f32[4,640]{1,0:T(4,128)} %bitcast.15, ...), custom_call_target="tpu_custom_call" | custom-call | tf_op jit(solution)/shard_map/mixer_section/pallas_call | solution.py:813
  101.7 1.7 %write_rows.1 = bf16[64,2560]{1,0:T(8,128)(2,1)} custom-call(bf16[64,2560]{1,0:T(8,128)(2,1)} %mixer_section.1.src), custom_call_target="tpu_custom_call" | custom-call | tf_op jit(solution)/shard_map/write_rows/pallas_call | solution.py:846

commit v7 on v6

--- a/solution.py
+++ b/solution.py
@@ -12,6 +12,11 @@
 F32 = jnp.float32
 BF16 = jnp.bfloat16
 MESH = pl.DeviceIdType.MESH
+
+
+def silu(v):
+    h = 0.5 * v
+    return h + h * jnp.tanh(h)
 
 
 def lanes_of(v, spread):
@@ -421,8 +426,8 @@
                 tap_x, tap_bc = keep * tap_x, keep * tap_bc
             run_x = run_x + tap_x * pre[at : at + 64, 0:el]
             run_bc = run_bc + tap_bc * pre[at : at + 64, el + 128 :]
-        xc[r0 : r0 + 64, :] = jax.nn.silu(run_x)
-        bcm[r0 : r0 + 64, :] = jax.nn.silu(run_bc).astype(BF16)
+        xc[r0 : r0 + 64, :] = silu(run_x)
+        bcm[r0 : r0 + 64, :] = silu(run_bc).astype(BF16)
 
     for r in range(1, toks // 64):
         convolve(r)
@@ -563,7 +568,7 @@
         seg = idc[8 + r0 : 8 + r0 + BLOCK, :]
         prev = idc[7 + r0 : 8 + r0, :]
         acc[rs, :] = acc[rs, :] + skip * xc[rs, :]
-        gate[rs, :] = jax.nn.silu(gate[rs, :])
+        gate[rs, :] = silu(gate[rs, :])
         xc[rs, :] = lanes_of(jnp.exp(ldb[b]) * jnp.where(seg == prev, 1.0, 0.0), spread)
 
     for copy in back_copies:

time: 104 us -> 104 us (level)
  no operation moved by 1% of the time
where the time goes in v7:
time: 104 us
  Pallas kernels  103 us (99%)
    pallas_call x1, Pallas kernels, local(): pl.pallas_call(functools.partial(layer_kernel, geo), out_shape=jax.ShapeD...  102 us

profile of v7, /device:TPU:1, one launch (start us, length us, event | category | flops | bytes accessed | tf_op | source)
XLA Modules:
  0.0 103.5 jit_solution(17355115685451980317)
XLA Ops:
  0.0 101.7 %mixer_section.1.src = bf16[64,2560]{1,0:T(8,128)(2,1)} custom-call(bf16[64,2560]{1,0:T(8,128)(2,1)} %bitcast.13, s32[1,512]{1,0:T(1,128)} %ids_ref.1, f32[1,2560]{1,0:T(1,128)} %norm_gain.1, bf16[2560,2,640]{2,1,0:T(2,128)(2,1)} %bitcast.10, bf16[2560,256]{1,0:T(8,128)(2,1)} %bitcast.12, bf16[10,2560]{1,0:T(8,128)(2,1)} %bitcast.14, f32[4,640]{1,0:T(4,128)} %bitcast.15, ...), custom_call_target="tpu_custom_call" | custom-call | tf_op jit(solution)/shard_map/mixer_section/pallas_call | solution.py:818
  101.7 1.7 %write_rows.1 = bf16[64,2560]{1,0:T(8,128)(2,1)} custom-call(bf16[64,2560]{1,0:T(8,128)(2,1)} %mixer_section.1.src), custom_call_target="tpu_custom_call" | custom-call | tf_op jit(solution)/shard_map/write_rows/pallas_call | solution.py:851
